TPU v7x, 8 devices: a whole 2x2x1 slice. The times are simulated.
8 devices in a mesh: rep: 1 (over z), dp: 8 (over x, y, core).
Axes of the slice: x: 2, y: 2, z: 1, core: 2. Of those that a mesh axis runs over, the one named last changes fastest.
Arguments:
- x: bfloat16 [8, 2048, 1024], P(('rep', 'dp'))
- dy: bfloat16 [8, 2048, 1024], P(('rep', 'dp'))
- w_gate: bfloat16 [2, 1024, 2816], replicated
- w_up: bfloat16 [2, 1024, 2816], replicated
- w_down: bfloat16 [2, 2816, 1024], replicated
- m_w_gate: float32 [2, 1024, 2816], replicated
- m_w_up: float32 [2, 1024, 2816], replicated
- m_w_down: float32 [2, 2816, 1024], replicated
- v_w_gate: float32 [2, 1024, 2816], replicated
- v_w_up: float32 [2, 1024, 2816], replicated
- v_w_down: float32 [2, 2816, 1024], replicated
Outputs:
- output 1: bfloat16 [2, 1024, 2816], P('rep')
- output 2: bfloat16 [2, 1024, 2816], P('rep')
- output 3: bfloat16 [2, 2816, 1024], P('rep')
- output 4: float32 [2, 1024, 2816], P('rep')
- output 5: float32 [2, 1024, 2816], P('rep')
- output 6: float32 [2, 2816, 1024], P('rep')
- output 7: float32 [2, 1024, 2816], P('rep')
- output 8: float32 [2, 1024, 2816], P('rep')
- output 9: float32 [2, 2816, 1024], P('rep')
All inputs are finite; a program needn't handle non-finite values.
Results may differ from a plain program's by a relative error of at most 0.022.
Values are sent between devices in bfloat16 or wider.
A program may use at most 2.75 GiB of HBM per device.

v0:
```python
import jax
import jax.numpy as jnp
from jax import lax
from jax.sharding import PartitionSpec as P

NAMES = ("w_gate", "w_up", "w_down")


def matmul(a, w):
    return jnp.dot(a, w, preferred_element_type=jnp.float32).astype(jnp.bfloat16)


def normed(h):
    wide = h.astype(jnp.float32)
    scale = lax.rsqrt(jnp.mean(wide**2, -1, keepdims=True) + 1e-6)
    return (wide * scale).astype(jnp.bfloat16)


def layer(h, w):
    a = normed(h)
    gate = jnp.dot(a, w["w_gate"], preferred_element_type=jnp.float32)
    up = jnp.dot(a, w["w_up"], preferred_element_type=jnp.float32)
    return h + matmul((jax.nn.silu(gate) * up).astype(jnp.bfloat16), w["w_down"])


def adamw(w, m, v, g):
    m = 0.9 * m + 0.1 * g
    v = 0.95 * v + 0.05 * g * g
    step = m * lax.rsqrt(v + 1e-8) + 0.1 * w
    return (w - 0.02 * step).astype(jnp.bfloat16), m, v


def clipped(gradients, sum_of_squares, count):
    factor = jnp.minimum(1.0, 0.5 * lax.rsqrt(sum_of_squares / count + 1e-30))
    return [g * factor for g in gradients]


def solution(mesh):
    def step(x, dy, *arrays):
        weights, m, v = (arrays[i : i + 3] for i in (0, 3, 6))
        layers = weights[0].shape[0]
        h, kept = x[0], []
        for number in range(layers):
            kept.append(h)
            h = layer(h, {name: w[number] for name, w in zip(NAMES, weights, strict=True)})
        by_h, summed = dy[0], [None] * layers
        for number in reversed(range(layers)):
            _, back = jax.vjp(lambda w, h: layer(h, w), {name: w[number] for name, w in zip(NAMES, weights, strict=True)}, kept[number])
            by_w, by_h = back(by_h)
            summed[number] = [lax.psum(by_w[name], "dp") for name in NAMES]
        gradients = [jnp.stack([summed[number][i] for number in range(layers)]).astype(jnp.float32) for i in range(3)]
        gradients = clipped(gradients, sum(jnp.sum(g * g) for g in gradients), sum(g.size for g in gradients))
        new = [adamw(w.astype(jnp.float32), m, v, g) for w, m, v, g in zip(weights, m, v, gradients, strict=True)]
        return tuple(one[which] for which in range(3) for one in new)

    return jax.shard_map(
        step,
        mesh=mesh,
        in_specs=(P(("rep", "dp"), None, None),) * 2 + (P(None, None, None),) * 9,
        out_specs=(P("rep", None, None),) * 9,
        check_vma=False,
    )
```

profile of v0, /device:TPU:0, one launch (start us, length us, event | category | flops | bytes accessed | tf_op | source)
XLA Modules:
  0.0 920.5 jit_solution(18297892953114742529)
XLA Ops:
  7.2 0.0 all-reduce.3.cloned.1.call-start
  7.2 6.5 copy.20
  13.7 3.1 fusion.36
  16.8 6.5 copy.21
  23.3 18.3 %convolution_convert_fusion.1 = bf16[2048,2816]{1,0:T(8,128)(2,1)} fusion(bf16[2,2816,1024]{2,1,0:T(8,128)(2,1)} %param.15, bf16[1,2048,1024]{2,1,0:T(8,128)(2,1)} %param.12), kind=kOutput, calls=%fused_computation.68 | convolution fusion | flops 11816927232 | bytes 21495808 | tf_op jit(solution)/shard_map/transpose(jvp())/dot_general | solution.py:10
  41.6 18.3 %fusion.56 = f32[2048,2816]{1,0:T(8,128)} fusion(bf16[2,1024,2816]{2,1,0:T(8,128)(2,1)} %param.13, bf16[1,2048,1024]{2,1,0:T(8,128)(2,1)S(1)} %copy-done.4, f32[2048]{0:T(1024)S(1)} %add_rsqrt_fusion), kind=kOutput, calls=%fused_computation.93 | convolution fusion | flops 11817451520 | bytes 33038336 | tf_op jit(solution)/shard_map/dot_general | solution.py:21
  59.9 28.7 %multiply_convert_fusion.1 = (bf16[2048,2816]{1,0:T(8,128)(2,1)}, f32[2048,2816]{1,0:T(8,128)}) fusion(f32[2048,2816]{1,0:T(8,128)} %fusion.56, bf16[2,1024,2816]{2,1,0:T(8,128)(2,1)} %param.14, bf16[1,2048,1024]{2,1,0:T(8,128)(2,1)} %param.11, f32[2048]{0:T(1024)S(1)} %add_rsqrt_fusion), kind=kOutput, calls=%fused_computation.53 | convolution fusion | flops 11852054528 | bytes 67641344 | tf_op jit(solution)/shard_map/dot_general | solution.py:22
  88.6 19.8 %fusion.40 = (f32[2048]{0:T(1024)S(1)}, bf16[2048,1024]{0,1:T(8,128)(2,1)}) fusion(bf16[2048,2816]{1,0:T(8,128)(2,1)} %get-tuple-element.24, bf16[2,2816,1024]{2,1,0:T(8,128)(2,1)} %param.15, bf16[1,2048,1024]{1,2,0:T(8,128)(2,1)} %copy.20), kind=kOutput, calls=%fused_computation.76 | convolution fusion | flops 11821643776 | bytes 25698304 | tf_op jit(solution)/shard_map/dot_general | solution.py:10
  108.5 0.6 copy-done.5
  109.0 20.3 %fusion.43 = f32[2048,2816]{1,0:T(8,128)} fusion(bf16[2,1024,2816]{2,1,0:T(8,128)(2,1)} %param.14, bf16[2048,1024]{0,1:T(8,128)(2,1)} %get-tuple-element.27, f32[2048]{0:T(1024)S(1)} %fusion.86), kind=kOutput, calls=%fused_computation.80 | convolution fusion | flops 11817451520 | bytes 33038336 | tf_op jit(solution)/shard_map/jvp()/dot_general | solution.py:22
  129.3 31.5 %fusion.20 = (bf16[2048,2816]{1,0:T(8,128)(2,1)}, f32[2048,2816]{1,0:T(8,128)}) fusion(f32[2048,2816]{1,0:T(8,128)} %fusion.43, bf16[2048,2816]{1,0:T(8,128)(2,1)} %convolution_convert_fusion.1, bf16[2,1024,2816]{2,1,0:T(8,128)(2,1)} %param.13, bf16[2048,1024]{0,1:T(8,128)(2,1)S(1)} %copy-done.1, f32[2048]{0:T(1024)S(1)} %fusion.86), kind=kOutput, calls=%fused_computation.41 | convolution fusion | flops 11886657536 | bytes 79175680 | tf_op jit(solution)/shard_map/jvp()/dot_general | solution.py:21
  160.8 20.2 %fusion.33 = bf16[2048,1024]{0,1:T(8,128)(2,1)} fusion(bf16[2048,2816]{1,0:T(8,128)(2,1)} %convolution_convert_fusion.1, bf16[2,1024,2816]{2,1,0:T(8,128)(2,1)} %param.14, f32[2048,2816]{1,0:T(8,128)} %get-tuple-element.29), kind=kOutput, calls=%fused_computation.57 | convolution fusion | flops 11845763072 | bytes 44564480 | tf_op jit(solution)/shard_map/transpose(jvp())/dot_general | solution.py:22
  181.0 22.4 %convert_bitcast_fusion.2 = bf16[1,1024,2816]{2,1,0:T(8,128)(2,1)} fusion(bf16[2048,2816]{1,0:T(8,128)(2,1)} %convolution_convert_fusion.1, bf16[2048,1024]{0,1:T(8,128)(2,1)} %get-tuple-element.27, f32[2048]{0:T(1024)S(1)} %fusion.86, f32[2048,2816]{1,0:T(8,128)} %get-tuple-element.29), kind=kOutput, calls=%fused_computation.97 | convolution fusion | flops 11854938112 | bytes 44572672 | tf_op jit(solution)/shard_map/transpose(jvp())/dot_general | solution.py:22
  203.4 23.8 %convert_bitcast_fusion = bf16[1,2816,1024]{2,1,0:T(8,128)(2,1)} fusion(f32[2048,2816]{1,0:T(8,128)} %fusion.43, bf16[1,2048,1024]{2,1,0:T(8,128)(2,1)} %param.12, f32[2048,2816]{1,0:T(8,128)} %get-tuple-element.29), kind=kOutput, calls=%fused_computation.95 | convolution fusion | flops 11848646656 | bytes 56098816 | tf_op jit(solution)/shard_map/transpose(jvp())/dot_general | solution.py:10
  227.2 17.5 %convert_bitcast_fusion.4 = bf16[1,1024,2816]{2,1,0:T(8,128)(2,1)} fusion(bf16[2048,2816]{1,0:T(8,128)(2,1)} %get-tuple-element.28, bf16[2048,1024]{0,1:T(8,128)(2,1)S(1)} %copy-done.2, f32[2048]{0:T(1024)S(1)} %fusion.86), kind=kOutput, calls=%fused_computation.99 | convolution fusion | flops 11817451520 | bytes 21504000 | tf_op jit(solution)/shard_map/transpose(jvp())/dot_general | solution.py:21
  244.7 19.6 %fusion.42 = (f32[2048]{0:T(1024)S(1)}, bf16[2048,1024]{0,1:T(8,128)(2,1)}) fusion(bf16[2048,1024]{0,1:T(8,128)(2,1)S(1)} %copy-done.2, bf16[2048,1024]{0,1:T(8,128)(2,1)} %fusion.33, bf16[2048,2816]{1,0:T(8,128)(2,1)} %get-tuple-element.28, bf16[2,1024,2816]{2,1,0:T(8,128)(2,1)} %param.13), kind=kOutput, calls=%fused_computation.78 | convolution fusion | flops 11821643776 | bytes 29892608 | tf_op jit(solution)/shard_map/transpose(jvp())/dot_general | solution.py:21
  264.4 6.0 fusion.70
  270.4 18.4 %convolution_convert_fusion = bf16[2048,2816]{1,0:T(8,128)(2,1)} fusion(bf16[2048,1024]{0,1:T(8,128)(2,1)} %fusion.70, bf16[2,2816,1024]{2,1,0:T(8,128)(2,1)} %param.15), kind=kOutput, calls=%fused_computation.67 | convolution fusion | flops 11816927232 | bytes 21495808 | tf_op jit(solution)/shard_map/transpose(jvp())/dot_general | solution.py:10
  288.8 17.0 %convert_bitcast_fusion.1 = bf16[1,2816,1024]{2,1,0:T(8,128)(2,1)} fusion(bf16[2048,2816]{1,0:T(8,128)(2,1)} %get-tuple-element.24, bf16[2048,1024]{0,1:T(8,128)(2,1)S(1)} %copy-done.3), kind=kOutput, calls=%fused_computation.96 | convolution fusion | flops 11814043648 | bytes 21495808 | tf_op jit(solution)/shard_map/transpose(jvp())/dot_general | solution.py:10
  305.8 0.0 copy-done.8
  305.8 22.3 %convert_bitcast_fusion.3 = bf16[1,1024,2816]{2,1,0:T(8,128)(2,1)} fusion(bf16[2048,2816]{1,0:T(8,128)(2,1)} %convolution_convert_fusion, f32[2048,2816]{1,0:T(8,128)} %fusion.56, bf16[1,2048,1024]{1,2,0:T(8,128)(2,1)} %copy.20, f32[2048]{0:T(1024)S(1)} %copy-done.8), kind=kOutput, calls=%fused_computation.98 | convolution fusion | flops 11854938112 | bytes 44572672 | tf_op jit(solution)/shard_map/transpose(jvp())/dot_general | solution.py:22
  328.1 26.9 %convert_bitcast_fusion.5 = bf16[1,1024,2816]{2,1,0:T(8,128)(2,1)} fusion(f32[2048,2816]{1,0:T(8,128)} %fusion.56, f32[2048,2816]{1,0:T(8,128)} %get-tuple-element.25, bf16[2048,2816]{1,0:T(8,128)(2,1)} %convolution_convert_fusion, bf16[1,2048,1024]{1,2,0:T(8,128)(2,1)} %copy.20, f32[2048]{0:T(1024)S(1)} %copy-done.8), kind=kOutput, calls=%fused_computation.100 | convolution fusion | flops 11883773952 | bytes 67641344 | tf_op jit(solution)/shard_map/transpose(jvp())/dot_general | solution.py:21
  355.0 0.0 all-reduce.3.cloned.1.call-update
  355.1 401.2 %all-reduce.3.cloned.1.call-done = (bf16[1,1024,2816]{2,1,0:T(8,128)(2,1)}, bf16[1,1024,2816]{2,1,0:T(8,128)(2,1)}, bf16[1,1024,2816]{2,1,0:T(8,128)(2,1)}, bf16...) async-done(((bf16[1,1024,2816]{2,1,0:T(8,128)(2,1)}, bf16[1,1024,2816]{2,1,0:T(8,128)(2,1)}, ...) | async-done | bytes 34603024 | tf_op jit(solution)/shard_map/psum | solution.py:50
  756.3 11.0 %fusion.10 = f32[]{:T(128)} fusion(bf16[1,1024,2816]{2,1,0:T(8,128)(2,1)} %get-tuple-element.9, bf16[1,1024,2816]{2,1,0:T(8,128)(2,1)} %get-tuple-element.10), kind=kLoop, calls=%fused_computation.31 | loop fusion | flops 23068672 | bytes 11534340 | tf_op jit(solution)/shard_map/reduce_sum | solution.py:52
  767.3 9.2 fusion.11
  777.8 0.0 slice-start
  777.8 11.2 %fusion.12 = f32[]{:T(128)} fusion(bf16[1,2816,1024]{2,1,0:T(8,128)(2,1)} %get-tuple-element.13, bf16[1,2816,1024]{2,1,0:T(8,128)(2,1)} %get-tuple-element.14), kind=kLoop, calls=%fused_computation.33 | loop fusion | flops 23068672 | bytes 11534340 | tf_op jit(solution)/shard_map/reduce_sum | solution.py:52
  789.7 0.0 slice-start.1
  789.7 40.7 %fusion.18 = (bf16[2,2816,1024]{2,1,0:T(8,128)(2,1)}, f32[2,2816,1024]{2,1,0:T(8,128)}, f32[2,2816,1024]{2,1,0:T(8,128)}) fusion(bf16[2,2816,1024]{2,1,0:T(8,128)(2,1)} %param.15, f32[]{:T(128)S(6)} %min_shard_map.3, bf16[1,2816,1024]{2,1,0:T(8,128)(2,1)} %get-tuple-element.13, bf16[1,2816,1024]{2,1,0:T(8,128)(2,1)} %get-tuple-element.14, ...), kind=kLoop, calls=%fused_computation.39 | loop fusion | flops 115343360 | bytes 126877696 | tf_op jit(solution)/shard_map/convert_element_type | solution.py:30
  830.4 0.0 slice-done
  830.4 82.7 %fusion.8 = (bf16[2,1024,2816]{2,1,0:T(8,128)(2,1)}, f32[2,1024,2816]{2,1,0:T(8,128)}, f32[2,1024,2816]{2,1,0:T(8,128)}, bf16[2,1024,2816]{2,1,0:T(8,128)(2,1)},...) fusion(bf16[2,1024,2816]{2,1,0:T(8,128)(2,1)} %param.13, f32[]{:T(128)S(6)} %min_shard_map.3, ...), kind=kLoop, calls=%fused_computation.29 | loop fusion | flops 230686720 | bytes 253755392 | tf_op jit(solution)/shard_map/convert_element_type | solution.py:30
  (26 shorter events, 0.1 us)
Async XLA Ops:
  7.2 749.1 %all-reduce.3.cloned.1.call-start = ((), (), s32[]{:S(2)}) async-start(), calls=%async_computation | async-start | bytes 69206016 | tf_op jit(solution)/shard_map/psum | solution.py:50
  16.8 43.1 %copy-start.7 = (f32[2048]{0:T(1024)}, f32[2048]{0:T(1024)S(1)}, u32[]{:S(2)}) copy-start(f32[2048]{0:T(1024)S(1)} %add_rsqrt_fusion) | copy-start | bytes 24580
  23.3 18.3 %copy-start.4 = (bf16[1,2048,1024]{2,1,0:T(8,128)(2,1)S(1)}, bf16[1,2048,1024]{2,1,0:T(8,128)(2,1)}, u32[]{:S(2)}) copy-start(bf16[1,2048,1024]{2,1,0:T(8,128)(2,1)} %param.11) | copy-start | bytes 12582916
  108.4 0.6 copy-start.5
  109.0 20.3 %copy-start.1 = (bf16[2048,1024]{0,1:T(8,128)(2,1)S(1)}, bf16[2048,1024]{0,1:T(8,128)(2,1)}, u32[]{:S(2)}) copy-start(bf16[2048,1024]{0,1:T(8,128)(2,1)} %get-tuple-element.27) | copy-start | bytes 12582916
  203.4 23.8 %copy-start.2 = (bf16[2048,1024]{0,1:T(8,128)(2,1)S(1)}, bf16[2048,1024]{0,1:T(8,128)(2,1)}, u32[]{:S(2)}) copy-start(bf16[2048,1024]{0,1:T(8,128)(2,1)} %get-tuple-element.27) | copy-start | bytes 12582916
  244.7 19.6 %copy-start.6 = (f32[2048]{0:T(1024)S(1)}, f32[2048]{0:T(1024)}, u32[]{:S(2)}) copy-start(f32[2048]{0:T(1024)} %copy-done.5) | copy-start | bytes 24580
  244.7 19.7 %copy-start = (bf16[1,2048,1024]{1,2,0:T(8,128)(2,1)S(1)}, bf16[1,2048,1024]{1,2,0:T(8,128)(2,1)}, u32[]{:S(2)}) copy-start(bf16[1,2048,1024]{1,2,0:T(8,128)(2,1)} %copy.21) | copy-start | bytes 12582916
  270.4 18.4 %copy-start.3 = (bf16[2048,1024]{0,1:T(8,128)(2,1)S(1)}, bf16[2048,1024]{0,1:T(8,128)(2,1)}, u32[]{:S(2)}) copy-start(bf16[2048,1024]{0,1:T(8,128)(2,1)} %fusion.70) | copy-start | bytes 12582916
  288.8 17.0 %copy-start.8 = (f32[2048]{0:T(1024)S(1)}, f32[2048]{0:T(1024)}, u32[]{:S(2)}) copy-start(f32[2048]{0:T(1024)} %copy-done.7) | copy-start | bytes 24580
  756.3 11.0 %slice-start.2 = ((s8[5767168]{0:T(1024)(128)(4,1)}), s8[4194304]{0:T(1024)(128)(4,1)S(1)}, s32[]{:S(2)}) async-start(s8[5767168]{0:T(1024)(128)(4,1)} %bitcast.76), calls=%async_computation.3 | async-start | bytes 8388608
  756.3 11.0 %slice-start.3 = ((s8[5767168]{0:T(1024)(128)(4,1)}), s8[1572864]{0:T(1024)(128)(4,1)S(1)}, s32[]{:S(2)}) async-start(s8[5767168]{0:T(1024)(128)(4,1)} %bitcast.76), calls=%async_computation.4 | async-start | bytes 3145728
  777.8 52.7 %slice-start = ((s8[5767168]{0:T(1024)(128)(4,1)}), s8[1572864]{0:T(1024)(128)(4,1)S(1)}, s32[]{:S(2)}) async-start(s8[5767168]{0:T(1024)(128)(4,1)} %bitcast.74), calls=%async_computation.1 | async-start | bytes 3145728
  789.7 40.7 %slice-start.1 = ((s8[5767168]{0:T(1024)(128)(4,1)}), s8[4194304]{0:T(1024)(128)(4,1)S(1)}, s32[]{:S(2)}) async-start(s8[5767168]{0:T(1024)(128)(4,1)} %bitcast.74), calls=%async_computation.2 | async-start | bytes 8388608
Sparse Core Ops, SparseCore 0:
  355.2 401.0 all-reduce.2
where the time goes:
time: 929 us; the launch traced here: 920 us
  waiting for transfers between devices  401 us (43%)
  matrix products  325 us (35%)
  other arithmetic  164 us (18%)
  between operations  16.6 us (2%)
  local copies, waits for them, and re-layouts  13.7 us (1%)
    psum x1, waiting for transfers between devices, step(): summed[number] = [lax.psum(by_w[name], 'dp') for name in NAMES]  401 us
    convert_element_type x2, other arithmetic, adamw(): return ((w - 0.02 * step).astype(jnp.bfloat16), m, v)  123 us
    dot_general x5, matrix products, layer(): up = jnp.dot(a, w['w_up'], preferred_element_type=jnp.float32)  114 us
    dot_general x5, matrix products, layer(): gate = jnp.dot(a, w['w_gate'], preferred_element_type=jnp.float32)  114 us
    dot_general x5, matrix products, matmul(): jnp.dot(a, w, preferred_element_type=jnp.float32).astype(jnp.bfloat16)  97.2 us
    reduce_sum x3, other arithmetic, step(): jnp.sum(g * g)  31.4 us
  transfers between devices with their start and end apart: 1, of which 1 were waited for; matrix products, arithmetic and copies ran while one was open for 0% of the time, Pallas kernels for 0%

commit v1 on v0

v1 whole, which is shorter than its diff:
```python
import functools

import jax
import jax.numpy as jnp
from jax import lax
from jax.experimental import pallas as pl
from jax.experimental.pallas import tpu as pltpu
from jax.sharding import PartitionSpec as P

T, D, F, TILE = 2048, 1024, 2816, 256
NT = F // TILE
BLOCK = 512
NB = T // BLOCK
DRAIN = 4
BF, F32 = jnp.bfloat16, jnp.float32
MESH = pl.DeviceIdType.MESH
VMEM_LIMIT = 62 * 1024 * 1024


def dot(a, b):
    return jnp.dot(a, b, preferred_element_type=F32)


def dot_t(a, b):
    return lax.dot_general(a, b, (((1,), (1,)), ((), ())), preferred_element_type=F32)


def whole(shape):
    zeros = (0,) * len(shape)
    return pl.BlockSpec(shape, lambda *_: zeros, pipeline_mode=pl.Buffered(1))


def scale_of(wide):
    return lax.rsqrt(jnp.mean(wide * wide, -1, keepdims=True) + 1e-6)


def forward_kernel(x_ref, dy_ref, wg_ref, wu_ref, wd_ref, gate_ref, up_ref, h_ref, a_ref, a0t_ref, at_ref, dyt_ref, a0, act):
    s = pl.program_id(0)

    @pl.when(s == 0)
    def _():
        for b in range(NB):
            rows = slice(b * BLOCK, (b + 1) * BLOCK)
            wide = x_ref[rows, :].astype(F32)
            a0[rows, :] = (wide * scale_of(wide)).astype(BF)

    @pl.when(s < NT)
    def _():
        columns = pl.ds(pl.multiple_of(s * TILE, TILE), TILE)
        wg, wu = wg_ref[0], wu_ref[0]
        for b in range(NB):
            rows = slice(b * BLOCK, (b + 1) * BLOCK)
            gate = dot(a0[rows, :], wg)
            up = dot(a0[rows, :], wu)
            gate_ref[rows, :] = gate
            up_ref[rows, :] = up
            act[rows, columns] = (gate * lax.logistic(gate) * up).astype(BF)

    @pl.when(s >= NT)
    def _():
        rows = pl.ds(pl.multiple_of((s - NT) * BLOCK, BLOCK), BLOCK)
        out = dot(act[rows, :], wd_ref[0]).astype(BF)
        h = (x_ref[rows, :].astype(F32) + out.astype(F32)).astype(BF)
        h_ref[...] = h
        wide = h.astype(F32)
        a = (wide * scale_of(wide)).astype(BF)
        a_ref[...] = a
        at_ref[...] = a.T
        a0t_ref[...] = a0[rows, :].T
        dyt_ref[...] = dy_ref[...].T


def forward(x, dy, wg, wu, wd):
    tile = lambda s: jnp.minimum(s, NT - 1)
    block = lambda s: jnp.maximum(s - NT, 0)
    wspec = pl.BlockSpec((1, D, TILE), lambda s: (0, 0, tile(s)))
    fspec = pl.BlockSpec((T, TILE), lambda s: (0, tile(s)))
    rspec = pl.BlockSpec((BLOCK, D), lambda s: (block(s), 0))
    tspec = pl.BlockSpec((D, BLOCK), lambda s: (0, block(s)))
    flat = lambda shape, dtype: jax.ShapeDtypeStruct(shape, dtype)
    return pl.pallas_call(
        forward_kernel,
        grid=(NT + NB,),
        in_specs=[whole((T, D)), rspec, wspec, wspec, whole((1, F, D))],
        out_specs=[fspec, fspec, rspec, rspec, tspec, tspec, tspec],
        out_shape=[
            flat((T, F), F32), flat((T, F), F32), flat((T, D), BF), flat((T, D), BF),
            flat((D, T), BF), flat((D, T), BF), flat((D, T), BF),
        ],
        scratch_shapes=[pltpu.VMEM((T, D), BF), pltpu.VMEM((T, F), BF)],
        compiler_params=pltpu.CompilerParams(dimension_semantics=("arbitrary",), vmem_limit_bytes=VMEM_LIMIT),
        cost_estimate=pl.CostEstimate(flops=6 * T * D * F, bytes_accessed=100 << 20, transcendentals=T * F),
        name="forward",
    )(x, dy, wg, wu, wd)


COMM_SCRATCH = [
    pltpu.VMEM((2, 4, 3, 128, 128), BF),
    pltpu.VMEM((2, 4, 3, 128, 128), F32),
    pltpu.VMEM((2, 2, 4, 3, 128, 128), BF),
    pltpu.VMEM((2, 2, 2, 3, 128, 128), BF),
    pltpu.VMEM((2, 2, 2, 3, 128, 128), F32),
    pltpu.VMEM((4, 2, 2, 3, 128, 128), BF),
    pltpu.VMEM((2, 2, 3, 128, 128), BF),
    pltpu.VMEM((2, 2, 3, 128, 128), F32),
    pltpu.VMEM((4, 2, 3, 128, 128), BF),
    pltpu.SemaphoreType.DMA((2,)),
    pltpu.SemaphoreType.DMA((2,)),
    pltpu.SemaphoreType.DMA((2, 2)),
    pltpu.SemaphoreType.DMA((4, 2)),
    pltpu.SemaphoreType.DMA((2, 2)),
    pltpu.SemaphoreType.DMA((4, 2)),
]


class Scatter:
    def __init__(self, refs, fin_ref, ssq_ref):
        (self.send_c, self.keep_c, self.recv_c, self.send_1, self.keep_1, self.recv_1, self.send_2, self.keep_2, self.recv_2,
         self.cs, self.cr, self.s1, self.r1, self.s2, self.r2) = refs
        self.fin_ref, self.ssq_ref = fin_ref, ssq_ref
        me = lax.axis_index("dp")
        self.core, self.y, self.x = lax.rem(me, 2), lax.rem(me // 2, 2), me // 4
        self.by_core, self.by_y, self.by_x = me + 1 - 2 * self.core, me + 2 - 4 * self.y, me + 4 - 8 * self.x

    def enter(self):
        barrier = pltpu.get_barrier_semaphore()
        for other in (self.by_core, self.by_y, self.by_x):
            pl.semaphore_signal(barrier, inc=1, device_id={"dp": other}, device_id_type=MESH)
        pl.semaphore_wait(barrier, 3)
        self.ssq_ref[...] = jnp.zeros_like(self.ssq_ref)

    def copy_c(self, t):
        slot = lax.rem(t, 2)
        return pltpu.make_async_remote_copy(
            self.send_c, self.recv_c.at[slot], self.cs.at[slot], self.cr.at[slot], device_id={"dp": self.by_core}, device_id_type=MESH)

    def copy_1(self, t, q):
        two, four = lax.rem(t, 2), lax.rem(t, 4)
        return pltpu.make_async_remote_copy(
            self.send_1.at[two, q], self.recv_1.at[four, q], self.s1.at[two, q], self.r1.at[four, q],
            device_id={"dp": self.by_y if q else self.by_x}, device_id_type=MESH)

    def copy_2(self, t, q):
        two, four = lax.rem(t, 2), lax.rem(t, 4)
        return pltpu.make_async_remote_copy(
            self.send_2.at[two, q], self.recv_2.at[four, q], self.s2.at[two, q], self.r2.at[four, q],
            device_id={"dp": self.by_x if q else self.by_y}, device_id_type=MESH)

    def middle(self, s):
        @pl.when((s >= 3) & (s <= NT + 2))
        def _():
            for q in range(2):
                self.copy_2(s - 3, q).start()

        @pl.when((s >= 1) & (s <= NT))
        def _():
            t = s - 1
            self.copy_c(t).wait()
            slot = lax.rem(t, 2)
            for q in range(2):
                mine = self.y if q else self.x
                for i in range(2):
                    away, here = 2 * (1 - mine) + i, 2 * mine + i
                    self.send_1[slot, q, i] = (self.keep_c[q, away] + self.recv_c[slot, q, away].astype(F32)).astype(BF)
                    self.keep_1[slot, q, i] = self.keep_c[q, here] + self.recv_c[slot, q, here].astype(F32)

    def end(self, s):
        @pl.when(s < NT)
        def _():
            self.copy_c(s).start()

        @pl.when((s >= 1) & (s <= NT))
        def _():
            for q in range(2):
                self.copy_1(s - 1, q).start()

        @pl.when(s >= 4)
        def _():
            t = s - 4
            two, four = lax.rem(t, 2), lax.rem(t, 4)
            squares = jnp.zeros((8, 128), F32)
            for q in range(2):
                self.copy_2(t, q).wait()
                g = (self.keep_2[two, q] + self.recv_2[four, q].astype(F32)).astype(BF)
                wide = g.astype(F32)
                squares += jnp.sum((wide * wide).reshape(48, 8, 128), 0)
                self.fin_ref[t, q, 0] = g[0]
                self.fin_ref[t, q, 1] = g[1]
                self.fin_ref[t, q, 2] = wide[2].T.astype(BF)
            self.ssq_ref[...] += squares

        @pl.when((s >= 2) & (s <= NT + 1))
        def _():
            t = s - 2
            two, four = lax.rem(t, 2), lax.rem(t, 4)
            for q in range(2):
                mine = self.x if q else self.y
                self.copy_1(t, q).wait()
                self.send_2[two, q] = (self.keep_1[two, q, 1 - mine] + self.recv_1[four, q, 1 - mine].astype(F32)).astype(BF)
                self.keep_2[two, q] = self.keep_1[two, q, mine] + self.recv_1[four, q, mine].astype(F32)

    def gradients(self, at_ref, dt_ref, dgate, dup, act):
        for half, to in ((1 - self.core, self.send_c), (self.core, self.keep_c)):
            rows = pl.ds(pl.multiple_of(half * 512, 512), 512)
            for i, (left, right) in enumerate(((at_ref, dgate), (at_ref, dup), (dt_ref, act))):
                out = dot(left[rows, :], right[...]).astype(to.dtype)
                for b in range(4):
                    for q in range(2):
                        to[q, b, i] = out[b * 128 : (b + 1) * 128, q * 128 : (q + 1) * 128]


def pieces(gate, up, dact):
    sig = lax.logistic(gate)
    silu = gate * sig
    dact = dact.astype(BF).astype(F32)
    act = (silu * up).astype(BF)
    dup = (dact * silu).astype(BF)
    dgate = (dact * up * (sig + silu * (1 - sig))).astype(BF)
    return act, dgate, dup


def backward_1_kernel(a_ref, dy_ref, at_ref, dyt_ref, h_ref, dyb_ref, wg_ref, wu_ref, wd_ref, fin_ref, ssq_ref, dh_ref, dht_ref, acc, act, dgate, dup, *comm):
    s = pl.program_id(0)
    scatter = Scatter(comm, fin_ref, ssq_ref)

    @pl.when(s == 0)
    def _():
        scatter.enter()
        acc[...] = jnp.zeros_like(acc)

    @pl.when(s < NT)
    def _():
        wg, wu, wd = wg_ref[0], wu_ref[0], wd_ref[0]
        for b in range(NB):
            rows = slice(b * BLOCK, (b + 1) * BLOCK)
            a = a_ref[rows, :]
            one, two, three = pieces(dot(a, wg), dot(a, wu), dot_t(dy_ref[rows, :], wd))
            act[rows, :], dgate[rows, :], dup[rows, :] = one, two, three
            acc[rows, :] += dot_t(two, wg) + dot_t(three, wu)

    scatter.middle(s)

    @pl.when(s < NT)
    def _():
        scatter.gradients(at_ref, dyt_ref, dgate, dup, act)

    @pl.when(s >= NT)
    def _():
        rows = pl.ds(pl.multiple_of((s - NT) * BLOCK, BLOCK), BLOCK)
        da = acc[rows, :].astype(BF).astype(F32)
        wide = h_ref[...].astype(F32)
        scale = scale_of(wide)
        inner = jnp.sum(da * wide, -1, keepdims=True)
        by_h = (da * scale - wide * (inner * (scale * scale * scale) * (1.0 / D))).astype(BF)
        dh = (dyb_ref[...].astype(F32) + by_h.astype(F32)).astype(BF)
        dh_ref[...] = dh
        dht_ref[...] = dh.T

    scatter.end(s)


def backward_0_kernel(dh_ref, at_ref, dht_ref, gate_ref, up_ref, wd_ref, fin_ref, ssq_ref, act, dgate, dup, *comm):
    s = pl.program_id(0)
    scatter = Scatter(comm, fin_ref, ssq_ref)

    @pl.when(s == 0)
    def _():
        scatter.enter()

    @pl.when(s < NT)
    def _():
        wd = wd_ref[0]
        for b in range(NB):
            rows = slice(b * BLOCK, (b + 1) * BLOCK)
            act[rows, :], dgate[rows, :], dup[rows, :] = pieces(gate_ref[rows, :], up_ref[rows, :], dot_t(dh_ref[rows, :], wd))

    scatter.middle(s)

    @pl.when(s < NT)
    def _():
        scatter.gradients(at_ref, dht_ref, dgate, dup, act)

    scatter.end(s)


FIN = jax.ShapeDtypeStruct((NT, 2, 3, 128, 128), BF)
SSQ = jax.ShapeDtypeStruct((8, 128), F32)


def backward(number, *operands):
    tile = lambda s: jnp.minimum(s, NT - 1)
    block = lambda s: jnp.clip(s - NT, 0, NB - 1)
    wspec = pl.BlockSpec((1, D, TILE), lambda s: (number, 0, tile(s)))
    dspec = pl.BlockSpec((1, TILE, D), lambda s: (number, tile(s), 0))
    fspec = pl.BlockSpec((T, TILE), lambda s: (0, tile(s)))
    rspec = pl.BlockSpec((BLOCK, D), lambda s: (block(s), 0))
    tspec = pl.BlockSpec((D, BLOCK), lambda s: (0, block(s)))
    out_shape, out_specs = [FIN, SSQ], [pl.BlockSpec(FIN.shape, lambda s: (0,) * 5), pl.BlockSpec((8, 128), lambda s: (0, 0))]
    scratch = [pltpu.VMEM((T, TILE), BF)] * 3
    if number == 1:
        kernel = backward_1_kernel
        in_specs = [whole((T, D)), whole((T, D)), whole((D, T)), whole((D, T)), rspec, rspec, wspec, wspec, dspec]
        out_shape += [jax.ShapeDtypeStruct((T, D), BF), jax.ShapeDtypeStruct((D, T), BF)]
        out_specs += [rspec, tspec]
        scratch = [pltpu.VMEM((T, D), F32)] + scratch
    else:
        kernel = backward_0_kernel
        in_specs = [whole((T, D)), whole((D, T)), whole((D, T)), fspec, fspec, dspec]
    return pl.pallas_call(
        kernel,
        grid=(NT + DRAIN,),
        in_specs=in_specs,
        out_specs=out_specs,
        out_shape=out_shape,
        scratch_shapes=scratch + COMM_SCRATCH,
        compiler_params=pltpu.CompilerParams(
            dimension_semantics=("arbitrary",), vmem_limit_bytes=VMEM_LIMIT, collective_id=number, has_side_effects=True),
        cost_estimate=pl.CostEstimate(flops=(16 if number else 8) * T * D * F, bytes_accessed=64 << 20, transcendentals=T * F),
        name=f"backward_{number}",
    )(*operands)


def owner(q, b):
    core, high, low = b // 4, (b // 2) % 2, b % 2
    x, y = (low, high) if q else (high, low)
    return 4 * x + 2 * y + core


def optimizer_kernel(n_alias, factor_ref, g_ref, *refs):
    ins, outs = refs[:9], refs[9 + n_alias :]
    factor = factor_ref[0, 0]
    for b in range(8):
        for q in range(2):
            for i in range(3):
                g = g_ref[owner(q, b), 0, q, i].astype(F32) * factor
                rows, columns = slice(b * 128, (b + 1) * 128), slice(q * 128, (q + 1) * 128)
                at = (0, columns, rows) if i == 2 else (0, rows, columns)
                w, m, v = (ins[3 * k + i][at] for k in range(3))
                m = 0.9 * m + 0.1 * g
                v = 0.95 * v + 0.05 * g * g
                w = w.astype(F32)
                w = (w - 0.02 * (m * lax.rsqrt(v + 1e-8) + 0.1 * w)).astype(BF)
                outs[i][at], outs[3 + i][at], outs[6 + i][at] = w, m, v


def optimizer(number, first, count, factor, g, arrays, so_far):
    wide = pl.BlockSpec((1, D, TILE), lambda s: (number, 0, first + s))
    tall = pl.BlockSpec((1, TILE, D), lambda s: (number, first + s, 0))
    three = [wide, wide, tall]
    so_far = list(so_far or ())
    out_shape = [jax.ShapeDtypeStruct(a.shape, a.dtype) for a in arrays]
    return pl.pallas_call(
        functools.partial(optimizer_kernel, len(so_far)),
        grid=(count,),
        in_specs=[pl.BlockSpec(memory_space=pltpu.SMEM), pl.BlockSpec((8, 1, 2, 3, 128, 128), lambda s: (0, s, 0, 0, 0, 0))]
        + three * 3 + [pl.BlockSpec(memory_space=pl.ANY)] * len(so_far),
        out_specs=three * 3,
        out_shape=out_shape,
        input_output_aliases={11 + i: i for i in range(len(so_far))},
        compiler_params=pltpu.CompilerParams(dimension_semantics=("arbitrary",), vmem_limit_bytes=VMEM_LIMIT),
        cost_estimate=pl.CostEstimate(flops=count * 20 * 3 * D * TILE, bytes_accessed=count * 22 * 3 * D * TILE, transcendentals=count * 3 * D * TILE),
        name=f"optimizer_{number}_{first}",
    )(factor, g, *arrays, *so_far)


def solution(mesh):
    def step(x, dy, *arrays):
        wg, wu, wd = arrays[:3]
        x, dy = x[0], dy[0]
        gate, up, h, a, a0t, at, dyt = forward(x, dy, wg, wu, wd)
        fin1, ssq1, dh, dht = backward(1, a, dy, at, dyt, h, dy, wg, wu, wd)
        fin0, ssq0 = backward(0, dh, a0t, dht, gate, up, wd)
        total = lax.psum(jnp.sum(ssq1 + ssq0), "dp")
        count = sum(w.size for w in arrays[:3])
        factor = jnp.minimum(1.0, 0.5 * lax.rsqrt(total / count + 1e-30)).reshape(1, 1)
        g1 = lax.all_gather(fin1, "dp")
        new = optimizer(1, 0, NT, factor, g1, arrays, None)
        cut = 5
        for first, count in ((0, cut), (cut, NT - cut)):
            g0 = lax.all_gather(fin0[first : first + count], "dp")
            new = optimizer(0, first, count, factor, g0, arrays, new)
        return tuple(new)

    return jax.shard_map(
        step,
        mesh=mesh,
        in_specs=(P(("rep", "dp"), None, None),) * 2 + (P(None, None, None),) * 9,
        out_specs=(P("rep", None, None),) * 9,
        check_vma=False,
    )
```

time: 929 us -> 521 us (0.56)
  Pallas kernels: 0 us -> 477 us
  waiting for transfers between devices: 401 us -> 0.11 us
  matrix products: 325 us -> 0 us
  other arithmetic: 164 us -> 1.28 us
  blocking collectives: 0 us -> 23 us
    pallas_call x0 -> x6, Pallas kernels: none -> 477 us  [the longest x2 299 us: backward(): pl.pallas_call(kernel, grid=(NT + DRAIN,), in_specs=in_specs, out_specs=o...]
    psum x1 -> x0, waiting for transfers between devices: 401 us -> none  [step(): summed[number] = [lax.psum(by_w[name], 'dp') for name in NAMES]]
    dot_general x15 -> x0, matrix products: 325 us -> none  [the longest x5 114 us: layer(): up = jnp.dot(a, w['w_up'], preferred_element_type=jnp.float32)]
    convert_element_type x2 -> x0, other arithmetic: 123 us -> none  [adamw(): return ((w - 0.02 * step).astype(jnp.bfloat16), m, v)]
    reduce_sum x4 -> x1, other arithmetic: 34.5 us -> 1.28 us  [step(): total = lax.psum(jnp.sum(ssq1 + ssq0), 'dp')]
    psum x0 -> x1, blocking collectives: none -> 23 us  [step(): total = lax.psum(jnp.sum(ssq1 + ssq0), 'dp')]
    unnamed x28 -> x2, local copies, waits for them, and re-layouts: 13.7 us -> 0.01 us
  transfers between devices with their start and end apart: 1 -> 3, of which waited for: 1 -> 0; matrix products, arithmetic and copies ran while one was open for 0% -> 1% of each run, Pallas kernels for 0% -> 47%
where the time goes in v1:
time: 521 us
  Pallas kernels  477 us (92%)
  blocking collectives  23 us (4%)
  between operations  14.5 us (3%)
    pallas_call x2, Pallas kernels, backward(): pl.pallas_call(kernel, grid=(NT + DRAIN,), in_specs=in_specs, out_specs=o...  299 us
    pallas_call x3, Pallas kernels, optimizer(): pl.pallas_call(functools.partial(optimizer_kernel, len(so_far)), grid=(co...  127 us
    pallas_call x1, Pallas kernels, forward(): pl.pallas_call(forward_kernel, grid=(NT + NB,), in_specs=[whole((T, D)),...  51.6 us
    psum x1, blocking collectives, step(): total = lax.psum(jnp.sum(ssq1 + ssq0), 'dp')  23 us
  transfers between devices with their start and end apart: 3, of which 0 were waited for; matrix products, arithmetic and copies ran while one was open for 1% of the time, Pallas kernels for 47%

profile of v1, /device:TPU:0, one launch (start us, length us, event | category | flops | bytes accessed | tf_op | source)
XLA Modules:
  0.0 521.1 jit_solution(2440033869998276658)
XLA Ops:
  7.2 0.0 all-gather.11.cloned.1.call-start
  7.2 51.6 %forward.1 = (f32[2048,2816]{1,0:T(8,128)}, f32[2048,2816]{1,0:T(8,128)}, bf16[2048,1024]{1,0:T(8,128)(2,1)}, bf16[2048,1024]{1,0:T(8,128)(2,1)}, bf16[1024,2048...) custom-call(bf16[2048,1024]{1,0:T(8,128)(2,1)} %bitcast.9, bf16[2048,1024]{1,0:T(8,128)(2,1)} %bitcast.10, ...), custom_call_target="tpu_custom_call" | custom-call | flops 35433480192 | bytes 104857600 | tf_op jit(solution)/shard_map/forward/pallas_call | solution.py:81
  58.9 148.3 %backward_1.1 = (bf16[11,2,3,128,128]{4,3,2,1,0:T(8,128)(2,1)}, f32[8,128]{1,0:T(8,128)}, bf16[2048,1024]{1,0:T(8,128)(2,1)}, bf16[1024,2048]{1,0:T(8,128)(2,1)}) custom-call(bf16[2048,1024]{1,0:T(8,128)(2,1)} %get-tuple-element.40.a_ref, bf16[2048,1024]{1,0:T(8,128)(2,1)} %bitcast.11, bf16[1024,2048]{1,0:T(8,128)(2,1)} %get-tuple-element.41.at_ref, ...), custom_call_target="tpu_custom_call" | custom-call | flops 94489280512 | bytes 67108864 | tf_op jit(solution)/shard_map/backward_1/pallas_call | solution.py:309
  207.2 0.0 all-gather.11.cloned.1.call-update
  207.2 0.0 all-gather.9.cloned.1.call-start
  207.2 0.0 copy-start
  207.2 150.8 %backward_0.1 = (bf16[11,2,3,128,128]{4,3,2,1,0:T(8,128)(2,1)}, f32[8,128]{1,0:T(8,128)}) custom-call(bf16[2048,1024]{1,0:T(8,128)(2,1)} %get-tuple-element.45.dh_ref, bf16[1024,2048]{1,0:T(8,128)(2,1)} %get-tuple-element.46.at_ref, bf16[1024,2048]{1,0:T(8,128)(2,1)} %get-tuple-element.47.dht_ref, f32[2048,2816]{1,0:T(8,128)} %get-tuple-element.48.gate_ref, ...), custom_call_target="tpu_custom_call" | custom-call | flops 47244640256 | bytes 67108864 | tf_op jit(solution)/shard_map/backward_0/pallas_call | solution.py:309
  358.0 2.3 slice.7
  360.3 0.0 all-gather.9.cloned.1.call-update
  360.3 0.0 all-gather.7.cloned.1.call-start
  360.4 2.4 slice.6
  362.8 0.0 all-gather.7.cloned.1.call-update
  362.8 0.0 copy-done
  362.8 1.3 add_reduce_fusion
  364.1 23.0 %psum.7 = f32[]{:T(128)} all-reduce(f32[]{:T(128)} %add_reduce_fusion), channel_id=1, replica_groups=mesh['rep'=1,'dp'=8] {'dp'}, use_global_device_ids=true, to_apply=%region_1.0 | all-reduce | flops 1 | bytes 8 | tf_op jit(solution)/shard_map/psum | solution.py:373
  387.8 0.0 all-gather.11.cloned.1.call-done
  387.9 63.1 %optimizer_1_0.1 = (bf16[2,1024,2816]{2,1,0:T(8,128)(2,1)}, bf16[2,1024,2816]{2,1,0:T(8,128)(2,1)}, bf16[2,2816,1024]{2,1,0:T(8,128)(2,1)}, f32[2,1024,2816]{2,1...) custom-call(f32[1,1]{1,0:T(1,128)} %bitcast.2.factor_ref, ...), custom_call_target="tpu_custom_call" | custom-call | flops 173015040 | bytes 190316544 | tf_op jit(solution)/shard_map/optimizer_1_0/pallas_call | solution.py:352
  451.0 0.0 all-gather.9.cloned.1.call-done
  451.0 30.5 %optimizer_0_0.1 = (bf16[2,1024,2816]{2,1,0:T(8,128)(2,1)}, bf16[2,1024,2816]{2,1,0:T(8,128)(2,1)}, bf16[2,2816,1024]{2,1,0:T(8,128)(2,1)}, f32[2,1024,2816]{2,1...) custom-call(f32[1,1]{1,0:T(1,128)} %bitcast.2.factor_ref, ...), custom_call_target="tpu_custom_call", output_to_operand_aliasing={{0}: (11, {}), {1}: (12, {}), {2}: (13, {}), {3}: (14, {}),... | custom-call | flops 78643200 | bytes 86507520 | tf_op jit(solution)/shard_map/optimizer_0_0/pallas_call | solution.py:352
  481.5 0.0 all-gather.7.cloned.1.call-done
  481.5 33.0 %optimizer_0_5.1 = (bf16[2,1024,2816]{2,1,0:T(8,128)(2,1)}, bf16[2,1024,2816]{2,1,0:T(8,128)(2,1)}, bf16[2,2816,1024]{2,1,0:T(8,128)(2,1)}, f32[2,1024,2816]{2,1...) custom-call(f32[1,1]{1,0:T(1,128)} %bitcast.2.factor_ref, ...), custom_call_target="tpu_custom_call", output_to_operand_aliasing={{0}: (11, {}), {1}: (12, {}), {2}: (13, {}), {3}: (14, {}),... | custom-call | flops 94371840 | bytes 103809024 | tf_op jit(solution)/shard_map/optimizer_0_5/pallas_call | solution.py:352
Async XLA Ops:
  7.2 380.7 %all-gather.11.cloned.1.call-start = ((), (), s32[]{:S(2)}) async-start(), calls=%async_computation.2 | async-start | bytes 19464192 | tf_op jit(solution)/shard_map/all_gather | solution.py:376
  207.2 243.8 %all-gather.9.cloned.1.call-start = ((), (), s32[]{:S(2)}) async-start(), calls=%async_computation.1 | async-start | bytes 8847360 | tf_op jit(solution)/shard_map/all_gather | solution.py:380
  207.2 155.6 %copy-start = (f32[8,128]{1,0:T(8,128)S(1)}, f32[8,128]{1,0:T(8,128)}, u32[]{:S(2)}) copy-start(f32[8,128]{1,0:T(8,128)} %get-tuple-element.44) | copy-start | bytes 12292
  360.3 121.2 %all-gather.7.cloned.1.call-start = ((), (), s32[]{:S(2)}) async-start(), calls=%async_computation | async-start | bytes 10616832 | tf_op jit(solution)/shard_map/all_gather | solution.py:380
Sparse Core Ops, SparseCore 0:
  207.3 145.3 all-gather.10
  360.4 47.2 all-gather.8
  409.5 52.9 all-gather.6

commit v2 on v1

v2 whole, which is shorter than its diff:
```python
import functools

import jax
import jax.numpy as jnp
from jax import lax
from jax.experimental import pallas as pl
from jax.experimental.pallas import tpu as pltpu
from jax.sharding import PartitionSpec as P


T, D, F, TILE = 2048, 1024, 2816, 256
NT = F // TILE
BLOCK = 512
CHUNK = 64
LANES = 128
PIECE = (3, LANES, LANES)
NB = T // BLOCK
DRAIN = 5
EARLY = 2
UNITS_1 = ((EARLY, 6), (6, NT))
UNITS_0 = ((0, 5), (5, NT))
STAGES = {10: "a0", 12: "a1", 15: "b0", 17: "b1", 20: "c0", 22: "c1 d0", 25: "d1"}
BF, F32 = jnp.bfloat16, jnp.float32
MESH = pl.DeviceIdType.MESH
VMEM_LIMIT = 62 * 1024 * 1024


def dot(a, b):
    return jnp.dot(a, b, preferred_element_type=F32)


def dot_t(a, b):
    return lax.dot_general(a, b, (((1,), (1,)), ((), ())), preferred_element_type=F32)


def whole(shape):
    zeros = (0,) * len(shape)
    return pl.BlockSpec(shape, lambda *_: zeros, pipeline_mode=pl.Buffered(1))


def scale_of(wide):
    return lax.rsqrt(jnp.mean(wide * wide, -1, keepdims=True) + 1e-6)


def forward_kernel(x_ref, dy_ref, wg_ref, wu_ref, wd_ref, gate_ref, up_ref, h_ref, a_ref, a0t_ref, at_ref, dyt_ref, a0, act, wd, sem):
    s = pl.program_id(0)
    load = pltpu.make_async_copy(wd_ref.at[0], wd, sem)

    @pl.when(s == 0)
    def _():
        load.start()
        for b in range(NB):
            rows = slice(b * BLOCK, (b + 1) * BLOCK)
            wide = x_ref[rows, :].astype(F32)
            a0[rows, :] = (wide * scale_of(wide)).astype(BF)

    @pl.when(s < NT)
    def _():
        columns = pl.ds(pl.multiple_of(s * TILE, TILE), TILE)
        wg, wu = wg_ref[0], wu_ref[0]
        for b in range(NB):
            rows = slice(b * BLOCK, (b + 1) * BLOCK)
            gate = dot(a0[rows, :], wg)
            up = dot(a0[rows, :], wu)
            gate_ref[0, rows, :] = gate
            up_ref[0, rows, :] = up
            act[rows, columns] = (gate * (0.5 * jnp.tanh(0.5 * gate) + 0.5) * up).astype(BF)

    @pl.when(s == NT)
    def _():
        load.wait()

    @pl.when(s >= NT)
    def _():
        rows = pl.ds(pl.multiple_of((s - NT) * BLOCK, BLOCK), BLOCK)
        out = dot(act[rows, :], wd[...]).astype(BF)
        h = (x_ref[rows, :].astype(F32) + out.astype(F32)).astype(BF)
        h_ref[...] = h
        wide = h.astype(F32)
        a = (wide * scale_of(wide)).astype(BF)
        a_ref[...] = a
        at_ref[...] = a.T
        a0t_ref[...] = a0[rows, :].T
        dyt_ref[...] = dy_ref[...].T


def forward(x, dy, wg, wu, wd):
    tile = lambda s: jnp.minimum(s, NT - 1)
    block = lambda s: jnp.maximum(s - NT, 0)
    wspec = pl.BlockSpec((1, D, TILE), lambda s: (0, 0, tile(s)))
    fspec = pl.BlockSpec((1, T, TILE), lambda s: (tile(s), 0, 0))
    rspec = pl.BlockSpec((BLOCK, D), lambda s: (block(s), 0))
    tspec = pl.BlockSpec((D, BLOCK), lambda s: (0, block(s)))
    flat = lambda shape, dtype: jax.ShapeDtypeStruct(shape, dtype)
    return pl.pallas_call(
        forward_kernel,
        grid=(NT + NB,),
        in_specs=[whole((T, D)), rspec, wspec, wspec, pl.BlockSpec(memory_space=pl.ANY)],
        out_specs=[fspec, fspec, rspec, rspec, tspec, tspec, tspec],
        out_shape=[
            flat((NT, T, TILE), F32), flat((NT, T, TILE), F32), flat((T, D), BF), flat((T, D), BF),
            flat((D, T), BF), flat((D, T), BF), flat((D, T), BF),
        ],
        scratch_shapes=[pltpu.VMEM((T, D), BF), pltpu.VMEM((T, F), BF), pltpu.VMEM((F, D), BF), pltpu.SemaphoreType.DMA],
        compiler_params=pltpu.CompilerParams(dimension_semantics=("arbitrary",), vmem_limit_bytes=VMEM_LIMIT),
        cost_estimate=pl.CostEstimate(flops=6 * T * D * F, bytes_accessed=100 << 20, transcendentals=T * F),
        name="forward",
    )(x, dy, wg, wu, wd)


COMM_SCRATCH = [
    pltpu.VMEM((2, 4, *PIECE), BF),
    pltpu.VMEM((2, 4, *PIECE), F32),
    pltpu.VMEM((2, 2, 4, *PIECE), BF),
    pltpu.VMEM((2, 2, 2, *PIECE), BF),
    pltpu.VMEM((2, 2, 2, *PIECE), F32),
    pltpu.VMEM((4, 2, 2, *PIECE), BF),
    pltpu.VMEM((2, 2, *PIECE), BF),
    pltpu.VMEM((2, 2, *PIECE), F32),
    pltpu.VMEM((4, 2, *PIECE), BF),
    pltpu.SemaphoreType.DMA((2,)),
    pltpu.SemaphoreType.DMA((2,)),
    pltpu.SemaphoreType.DMA((2, 2)),
    pltpu.SemaphoreType.DMA((4, 2)),
    pltpu.SemaphoreType.DMA((2, 2)),
    pltpu.SemaphoreType.DMA((4, 2)),
]


class Scatter:
    def __init__(self, refs, place, ssq_ref):
        (self.send_c, self.keep_c, self.recv_c, self.send_1, self.keep_1, self.recv_1, self.send_2, self.keep_2, self.recv_2,
         self.cs, self.cr, self.s1, self.r1, self.s2, self.r2) = refs
        self.place, self.ssq_ref = place, ssq_ref
        me = lax.axis_index("dp")
        self.core, self.y, self.x = lax.rem(me, 2), lax.rem(me // 2, 2), me // 4
        self.by_core, self.by_y, self.by_x = me + 1 - 2 * self.core, me + 2 - 4 * self.y, me + 4 - 8 * self.x

    def enter(self, others):
        barrier = pltpu.get_barrier_semaphore()
        for other in others:
            pl.semaphore_signal(barrier, inc=1, device_id={"dp": other}, device_id_type=MESH)
        pl.semaphore_wait(barrier, len(others))

    def copy_c(self, t):
        slot = lax.rem(t, 2)
        return pltpu.make_async_remote_copy(
            self.send_c, self.recv_c.at[slot], self.cs.at[slot], self.cr.at[slot], device_id={"dp": self.by_core}, device_id_type=MESH)

    def copy_1(self, t, q):
        two, four = lax.rem(t, 2), lax.rem(t, 4)
        return pltpu.make_async_remote_copy(
            self.send_1.at[two, q], self.recv_1.at[four, q], self.s1.at[two, q], self.r1.at[four, q],
            device_id={"dp": self.by_y if q else self.by_x}, device_id_type=MESH)

    def copy_2(self, t, q):
        two, four = lax.rem(t, 2), lax.rem(t, 4)
        return pltpu.make_async_remote_copy(
            self.send_2.at[two, q], self.recv_2.at[four, q], self.s2.at[two, q], self.r2.at[four, q],
            device_id={"dp": self.by_x if q else self.by_y}, device_id_type=MESH)

    def on(self, t):
        return pl.when((t >= 0) & (t < NT))

    def sums(self, first, second, third):
        @self.on(third)
        def _():
            t, two, four = third, lax.rem(third, 2), lax.rem(third, 4)
            squares = jnp.zeros((8, LANES), F32)
            for q in range(2):
                self.copy_2(t, q).wait()
                g = (self.keep_2[two, q] + self.recv_2[four, q].astype(F32)).astype(BF)
                wide = g.astype(F32)
                squares += jnp.sum((wide * wide).reshape(48, 8, LANES), 0)
                for start, stop, ref in self.place:

                    @pl.when((t >= start) & (t < stop))
                    def _():
                        ref[q, t - start, 0] = g[0]
                        ref[q, t - start, 1] = g[1]
                        ref[q, t - start, 2] = wide[2].T.astype(BF)

            self.ssq_ref[...] += squares

        @self.on(second)
        def _():
            two, four = lax.rem(second, 2), lax.rem(second, 4)
            for q in range(2):
                mine = self.x if q else self.y
                self.copy_1(second, q).wait()
                self.send_2[two, q] = (self.keep_1[two, q, 1 - mine] + self.recv_1[four, q, 1 - mine].astype(F32)).astype(BF)
                self.keep_2[two, q] = self.keep_1[two, q, mine] + self.recv_1[four, q, mine].astype(F32)

        @self.on(first)
        def _():
            self.copy_c(first).wait()
            slot = lax.rem(first, 2)
            for q in range(2):
                mine = self.y if q else self.x
                for i in range(2):
                    away, here = 2 * (1 - mine) + i, 2 * mine + i
                    self.send_1[slot, q, i] = (self.keep_c[q, away] + self.recv_c[slot, q, away].astype(F32)).astype(BF)
                    self.keep_1[slot, q, i] = self.keep_c[q, here] + self.recv_c[slot, q, here].astype(F32)

    def sends(self, first, second):
        @self.on(first)
        def _():
            for q in range(2):
                self.copy_1(first, q).start()

        @self.on(second)
        def _():
            for q in range(2):
                self.copy_2(second, q).start()

    def gradients(self, at_ref, dt_ref, dgate, dup, act, between=lambda: None):
        for half, to in ((1 - self.core, self.send_c), (self.core, self.keep_c)):
            rows = pl.ds(pl.multiple_of(half * 512, 512), 512)
            for i, (left, right) in enumerate(((at_ref, dgate), (at_ref, dup), (dt_ref, act))):
                out = dot(left[rows, :], right[...]).astype(to.dtype)
                for b in range(4):
                    for q in range(2):
                        to[q, b, i] = out[b * LANES : (b + 1) * LANES, q * LANES : (q + 1) * LANES]
            if to is self.send_c:
                between()


class Gather:
    def __init__(self, scatter, fin, g_ref, la, sa, ra, sb, rb, sc, rc):
        self.s, self.fin, self.g = scatter, fin, g_ref
        self.sems = la, sa, ra, sb, rb, sc, rc
        x, y, core = scatter.x, scatter.y, scatter.core
        self.mine = (4 * core + 2 * x + y, 4 * core + 2 * y + x)
        self.pair = (4 * core + 2 * x, 4 * core + 2 * y)

    def local(self, t, q):
        return pltpu.make_async_copy(self.fin.at[q, t], self.g.at[t, q, self.mine[q]], self.sems[0].at[t, q])

    def remote(self, t, q, source, target, sems, to):
        send, receive = sems
        return pltpu.make_async_remote_copy(source, target, send.at[t, q], receive.at[t, q], device_id={"dp": to}, device_id_type=MESH)

    def a(self, t, q):
        here = self.g.at[t, q, self.mine[q]]
        return self.remote(t, q, self.fin.at[q, t], here, self.sems[1:3], self.s.by_x if q else self.s.by_y)

    def b(self, t, q):
        here = self.g.at[t, q, pl.ds(self.pair[q], 2)]
        return self.remote(t, q, here, here, self.sems[3:5], self.s.by_y if q else self.s.by_x)

    def c(self, t, q):
        here = self.g.at[t, q, pl.ds(4 * self.s.core, 4)]
        return self.remote(t, q, here, here, self.sems[5:7], self.s.by_core)

    def step(self, s):
        for at, events in STAGES.items():

            @pl.when(s == at)
            def _():
                for stage, t in events.split():
                    t = int(t)
                    for q in range(2):
                        if stage == "a":
                            self.local(t, q).start()
                            self.a(t, q).start()
                        elif stage == "b":
                            self.local(t, q).wait()
                            self.a(t, q).wait()
                            self.b(t, q).start()
                        elif stage == "c":
                            self.b(t, q).wait()
                            self.c(t, q).start()
                        else:
                            self.c(t, q).wait()


def pieces(gate, up, dact):
    sig = 0.5 * jnp.tanh(0.5 * gate) + 0.5
    silu = gate * sig
    dact = dact.astype(BF).astype(F32)
    act = (silu * up).astype(BF)
    dup = (dact * silu).astype(BF)
    dgate = (dact * up * (sig + silu * (1 - sig))).astype(BF)
    return act, dgate, dup


def backward_1_kernel(
    a_hbm, dy_hbm, at_hbm, dyt_hbm, h_ref, dyb_ref, wg_ref, wu_ref, wd_ref,
    *refs,
):
    fins, refs = refs[: len(UNITS_1)], refs[len(UNITS_1) :]
    (g_ref, ssq_ref, dh_ref, dht_ref, kept,
     a_ref, dy_ref, at_ref, dyt_ref, loads, acc, act, dgate, dup, again, saves, reads, fin, la, sa, ra, sb, rb, sc, rc, *comm) = refs
    s = pl.program_id(0)
    scatter = Scatter(comm, [(0, EARLY, fin)] + [(*unit, ref) for unit, ref in zip(UNITS_1, fins, strict=True)], ssq_ref)
    gather = Gather(scatter, fin, g_ref, la, sa, ra, sb, rb, sc, rc)
    load = [
        pltpu.make_async_copy(source, target, loads.at[i])
        for i, (source, target) in enumerate(((a_hbm, a_ref), (dy_hbm, dy_ref), (at_hbm, at_ref), (dyt_hbm, dyt_ref)))
    ]

    def save(t, i, source):
        return pltpu.make_async_copy(source, kept.at[t, i], saves.at[i])

    def read(t):
        slot = lax.rem(t, 2)
        return pltpu.make_async_copy(kept.at[t], again.at[slot], reads.at[slot])

    @pl.when(s == 0)
    def _():
        for one in load:
            one.start()
        acc[...] = jnp.zeros_like(acc)
        ssq_ref[...] = jnp.zeros_like(ssq_ref)
        scatter.enter((scatter.by_core, scatter.by_y, scatter.by_x))
        load[0].wait()
        load[1].wait()

    @pl.when(s < NT)
    def _():
        wg, wu, wd = wg_ref[0], wu_ref[0], wd_ref[0]
        for b in range(NB):
            rows = slice(b * BLOCK, (b + 1) * BLOCK)
            a = a_ref[rows, :]
            one, two, three = pieces(dot(a, wg), dot(a, wu), dot_t(dy_ref[rows, :], wd))
            act[rows, :], dgate[rows, :], dup[rows, :] = one, two, three

    @pl.when(s == 0)
    def _():
        load[2].wait()
        load[3].wait()

    @pl.when(s < NT)
    def _():
        scatter.sums(s - 1, s - 3, s - 5)
        for i, source in enumerate((dgate, dup)):
            save(s, i, source).start()
        scatter.gradients(at_ref, dyt_ref, dgate, dup, act)
        for i, source in enumerate((dgate, dup)):
            save(s, i, source).wait()
        scatter.copy_c(s).start()
        scatter.sends(s - 1, s - 3)

    @pl.when((s >= NT - 1) & (s < 2 * NT - 1))
    def _():
        read(s - (NT - 1)).start()

    @pl.when((s >= NT) & (s < 2 * NT))
    def _():
        tile = s - NT
        read(tile).wait()
        slot = lax.rem(tile, 2)
        both = jnp.concatenate([wg_ref[0], wu_ref[0]], 1)
        for b in range(NB):
            rows = slice(b * BLOCK, (b + 1) * BLOCK)
            acc[rows, :] += dot_t(jnp.concatenate([again[slot, 0, rows, :], again[slot, 1, rows, :]], 1), both)

        @pl.when((lax.rem(tile, 2) == 1) & (tile < 2 * DRAIN))
        def _():
            later = NT + tile // 2
            scatter.sums(later - 1, later - 3, later - 5)
            scatter.sends(later - 1, later - 3)

    @pl.when(s >= 2 * NT)
    def _():
        rows = pl.ds(pl.multiple_of((s - 2 * NT) * BLOCK, BLOCK), BLOCK)
        da = acc[rows, :].astype(BF).astype(F32)
        wide = h_ref[...].astype(F32)
        scale = scale_of(wide)
        inner = jnp.sum(da * wide, -1, keepdims=True)
        by_h = (da * scale - wide * (inner * (scale * scale * scale) * (1.0 / D))).astype(BF)
        dh = (dyb_ref[...].astype(F32) + by_h.astype(F32)).astype(BF)
        dh_ref[...] = dh
        dht_ref[...] = dh.T

    gather.step(s)


def backward_0_kernel(count, dh_hbm, at_hbm, dht_hbm, gate_ref, up_ref, wd_ref, ssq_1_ref, *refs):
    s = pl.program_id(0)
    fins, refs = refs[: len(UNITS_0)], refs[len(UNITS_0) :]
    factor_ref, dh_ref, at_ref, dht_ref, loads, act, dgate, dup, ssq, send, recv, squares, *comm = refs
    scatter = Scatter(comm, [(*unit, ref) for unit, ref in zip(UNITS_0, fins, strict=True)], ssq)
    load = [
        pltpu.make_async_copy(source, target, loads.at[i])
        for i, (source, target) in enumerate(((dh_hbm, dh_ref), (at_hbm, at_ref), (dht_hbm, dht_ref)))
    ]
    me = lax.axis_index("dp")
    others = [lax.rem(me + i, 8) for i in range(1, 8)]

    def tell(i):
        return pltpu.make_async_remote_copy(
            ssq, squares.at[me], send.at[i], recv.at[me], device_id={"dp": others[i]}, device_id_type=MESH)

    def hear(i):
        return pltpu.make_async_remote_copy(
            ssq, squares.at[others[i]], send.at[i], recv.at[others[i]], device_id={"dp": others[i]}, device_id_type=MESH)

    @pl.when(s == 0)
    def _():
        for one in load:
            one.start()
        ssq[...] = ssq_1_ref[...]
        scatter.enter(others)
        load[0].wait()

    @pl.when(s < NT)
    def _():
        wd = wd_ref[0]
        for b in range(NB):
            rows = slice(b * BLOCK, (b + 1) * BLOCK)
            act[rows, :], dgate[rows, :], dup[rows, :] = pieces(gate_ref[0, rows, :], up_ref[0, rows, :], dot_t(dh_ref[rows, :], wd))

    @pl.when(s == 0)
    def _():
        load[1].wait()
        load[2].wait()

    scatter.sums(s - 1, s - 3, s - 5)

    @pl.when(s < NT)
    def _():
        scatter.gradients(at_ref, dht_ref, dgate, dup, act)
        scatter.copy_c(s).start()

    scatter.sends(s - 1, s - 3)

    @pl.when(s == NT + DRAIN - 1)
    def _():
        for i in range(7):
            tell(i).start()
        squares[me] = ssq[...]
        for i in range(7):
            tell(i).wait_send()
            hear(i).wait_recv()
        total = squares[0]
        for i in range(1, 8):
            total += squares[i]
        total = jnp.broadcast_to(jnp.sum(total, keepdims=True), (8, LANES))
        factor_ref[...] = jnp.minimum(1.0, 0.5 * lax.rsqrt(total / count + 1e-30))


def backward(number, *operands):
    steps = 2 * NT + NB if number else NT + DRAIN
    tile = lambda s: jnp.minimum(s, NT - 1)
    twice = lambda s: jnp.where(s < NT, s, jnp.minimum(s - NT, NT - 1))
    block = lambda s: jnp.clip(s - 2 * NT, 0, NB - 1)
    anywhere = pl.BlockSpec(memory_space=pl.ANY)
    wspec = pl.BlockSpec((1, D, TILE), lambda s: (number, 0, twice(s)))
    dspec = pl.BlockSpec((1, TILE, D), lambda s: (number, tile(s), 0))
    fspec = pl.BlockSpec((1, T, TILE), lambda s: (tile(s), 0, 0))
    rspec = pl.BlockSpec((BLOCK, D), lambda s: (block(s), 0))
    tspec = pl.BlockSpec((D, BLOCK), lambda s: (0, block(s)))
    small = pl.BlockSpec((8, LANES), lambda s: (0, 0))
    shape = jax.ShapeDtypeStruct
    fin = [shape((2, last - first, *PIECE), BF) for first, last in (UNITS_1 if number else UNITS_0)]
    fins = [pl.BlockSpec(one.shape, lambda s: (0, 0, 0, 0, 0)) for one in fin]
    dma = pltpu.SemaphoreType.DMA
    scratch = [pltpu.VMEM((T, TILE), BF)] * 3
    if number == 1:
        kernel = backward_1_kernel
        in_specs = [anywhere] * 4 + [rspec, rspec, wspec, wspec, dspec]
        out_shape = fin + [
            shape((EARLY, 2, 8, *PIECE), BF), shape((8, LANES), F32), shape((T, D), BF), shape((D, T), BF), shape((NT, 2, T, TILE), BF)]
        out_specs = fins + [anywhere, small, rspec, tspec, anywhere]
        scratch = (
            [pltpu.VMEM((T, D), BF)] * 2 + [pltpu.VMEM((D, T), BF)] * 2 + [dma((4,)), pltpu.VMEM((T, D), F32)] + scratch
            + [pltpu.VMEM((2, 2, T, TILE), BF), dma((2,)), dma((2,))] + [pltpu.VMEM((2, EARLY, *PIECE), BF)] + [dma((EARLY, 2))] * 7 + COMM_SCRATCH
        )
    else:
        kernel = functools.partial(backward_0_kernel, float(2 * 3 * D * F))
        in_specs = [anywhere] * 3 + [fspec, fspec, dspec, small]
        out_shape, out_specs = fin + [shape((8, LANES), F32)], fins + [small]
        scratch = (
            [pltpu.VMEM((T, D), BF)] + [pltpu.VMEM((D, T), BF)] * 2 + [dma((3,))] + scratch
            + [pltpu.VMEM((8, LANES), F32), dma((7,)), dma((8,)), pltpu.VMEM((8, 8, LANES), F32)] + COMM_SCRATCH
        )
    return pl.pallas_call(
        kernel,
        grid=(steps,),
        in_specs=in_specs,
        out_specs=out_specs,
        out_shape=out_shape,
        scratch_shapes=scratch,
        compiler_params=pltpu.CompilerParams(
            dimension_semantics=("arbitrary",), vmem_limit_bytes=VMEM_LIMIT, collective_id=number, has_side_effects=True),
        cost_estimate=pl.CostEstimate(flops=(16 if number else 8) * T * D * F, bytes_accessed=64 << 20, transcendentals=T * F),
    )(*operands)


def optimizer_kernel(n_g, n_alias, factor_ref, *refs):
    gs, ins, outs = refs[:n_g], refs[n_g : n_g + 9], refs[n_g + 9 + n_alias :]
    factor = factor_ref[0:1, :]

    def update(g_ref, at_g, rows, columns):
        for i in range(3):
            g = g_ref[i, at_g].astype(F32) * factor
            at = (0, *(columns if i == 2 else rows))
            w, m, v = (ins[3 * k + i][at] for k in range(3))
            m = 0.9 * m + 0.1 * g
            v = 0.95 * v + 0.05 * g * g
            w = w.astype(F32)
            w = (w - 0.02 * (m * lax.rsqrt(v + 1e-8) + 0.1 * w)).astype(BF)
            outs[i][at], outs[3 + i][at], outs[6 + i][at] = w, m, v

    if n_g == 1:
        parts = [(gs[0].at[0, q, b], q, LANES * b) for b in range(8) for q in range(2)]
    else:
        me = lax.axis_index("dp")
        core, y, x = lax.rem(me, 2), lax.rem(me // 2, 2), me // 4
        parts = []
        for side in range(2):
            at_core = 1 - core if side else core
            for i, (far_y, far_x) in enumerate(SIDES):
                at_y, at_x = 1 - y if far_y else y, 1 - x if far_x else x
                for q in range(2):
                    g_ref = gs[5 * side + 3 + q].at[0] if i == 3 else gs[5 * side + i].at[q, 0]
                    parts.append((g_ref, q, pl.multiple_of(LANES * (4 * at_core + (2 * at_y + at_x if q else 2 * at_x + at_y)), LANES)))
    for g_ref, q, b in parts:

        @pl.loop(0, LANES // CHUNK)
        def _(c):
            at_g = pl.ds(pl.multiple_of(c * CHUNK, CHUNK), CHUNK)
            rows = pl.ds(pl.multiple_of(b + c * CHUNK, CHUNK), CHUNK), slice(q * LANES, (q + 1) * LANES)
            columns = pl.ds(pl.multiple_of(q * LANES + c * CHUNK, CHUNK), CHUNK), pl.ds(b, LANES)
            update(g_ref, at_g, rows, columns)


def optimizer(number, first, start, count, factor, gs, arrays, so_far):
    wide = pl.BlockSpec((1, D, TILE), lambda s: (number, 0, first + s))
    tall = pl.BlockSpec((1, TILE, D), lambda s: (number, first + s, 0))
    three = [wide, wide, tall]
    so_far = list(so_far or ())
    if len(gs) == 1:
        gspecs = [pl.BlockSpec((1, 2, 8, *PIECE), lambda s: (start + s, 0, 0, 0, 0, 0))]
    else:
        stacked = pl.BlockSpec((2, 1, *PIECE), lambda s: (0, start + s, 0, 0, 0))
        gspecs = ([stacked] * 3 + [pl.BlockSpec((1, *PIECE), lambda s: (start + s, 0, 0, 0))] * 2) * 2
    out_shape = [jax.ShapeDtypeStruct(a.shape, a.dtype) for a in arrays]
    return pl.pallas_call(
        functools.partial(optimizer_kernel, len(gs), len(so_far)),
        grid=(count,),
        in_specs=[pl.BlockSpec((8, LANES), lambda s: (0, 0))] + gspecs + three * 3 + [pl.BlockSpec(memory_space=pl.ANY)] * len(so_far),
        out_specs=three * 3,
        out_shape=out_shape,
        input_output_aliases={10 + len(gs) + i: i for i in range(len(so_far))},
        compiler_params=pltpu.CompilerParams(dimension_semantics=("arbitrary",), vmem_limit_bytes=VMEM_LIMIT),
        cost_estimate=pl.CostEstimate(flops=count * 6 * 10**8, bytes_accessed=count * 22 * 3 * D * TILE, transcendentals=count * 3 * D * TILE),
    )(factor, *gs, *arrays, *so_far)


SIDES = ((0, 0), (1, 0), (0, 1), (1, 1))

ONE, TWO, FAR = range(3)
PLAN = (
    (1, 0, 2, -1, [(TWO, 0), (ONE, 1)]),
    (1, 2, 4, 0, [(FAR, 0)]),
    (1, 4, 6, 0, [(TWO, 1), (ONE, 2)]),
    (1, 6, 9, 1, [(FAR, 1)]),
    (1, 9, 11, 1, [(TWO, 2), (ONE, 3)]),
    (0, 0, 3, 2, [(FAR, 2)]),
    (0, 3, 5, 2, [(TWO, 3)]),
    (0, 5, 11, 3, [(FAR, 3)]),
)


def swap(v, bit):
    return lax.ppermute(v, "dp", [(i, i ^ bit) for i in range(8)])


def solution(mesh):
    def step(x, dy, *arrays):
        wg, wu, wd = arrays[:3]
        x, dy = x[0], dy[0]
        gate, up, h, a, a0t, at, dyt = forward(x, dy, wg, wu, wd)
        *late, g1, ssq1, dh, dht, _ = backward(1, a, dy, at, dyt, h, dy, wg, wu, wd)
        one_hop = lambda v: [swap(v, 2), swap(v, 4)]
        other_core = lambda values: [swap(v, 1) for v in values]
        ahead = one_hop(late[0])
        *fin, factor = backward(0, dh, a0t, dht, gate, up, wd, ssq1)
        tie = lax.optimization_barrier
        late, ahead, factor = tie((late, ahead, factor))
        units = [(1, *unit) for unit in UNITS_1] + [(0, *unit) for unit in UNITS_0]
        own, one, two, far = late + fin, {0: ahead}, {}, {}

        far[0] = other_core([own[0]])
        new = None
        for number, first, last, u, opens in PLAN:
            if new:
                values = tie((new, [(own, one, two)[stage][i] for stage, i in opens]))
                new = values[0]
                for (stage, i), value in zip(opens, values[1], strict=True):
                    (own, one, two)[stage][i] = value
            for stage, i in opens:
                if stage == ONE:
                    one[i] = one_hop(own[i])
                    far[i] = other_core([own[i]])
                elif stage == TWO:
                    p, q = one[i][0][0], one[i][1][1]
                    two[i] = [swap(p, 4), swap(q, 2)]
                    far[i] = far[i] + other_core(one[i])
                else:
                    far[i] = far[i] + other_core(two[i])
            if u < 0:
                start, gs = first, [g1]
            else:
                start, gs = first - units[u][1], [own[u], *one[u], *two[u], *far[u]]
            new = optimizer(number, first, start, last - first, factor, gs, arrays, new)
        return tuple(new)

    return jax.shard_map(
        step,
        mesh=mesh,
        in_specs=(P(("rep", "dp"), None, None),) * 2 + (P(None, None, None),) * 9,
        out_specs=(P("rep", None, None),) * 9,
        check_vma=False,
    )
```

time: 521 us -> 494 us (0.948)
  Pallas kernels: 477 us -> 418 us
  waiting for transfers between devices: 0.11 us -> 41.2 us
  blocking collectives: 23 us -> 0 us
  starting transfers between devices: 0.12 us -> 22 us
  between operations: 14.5 us -> 1.12 us
  local copies, waits for them, and re-layouts: 4.7 us -> 10.8 us
    pallas_call x5 -> x10, Pallas kernels: 426 us -> 368 us  [the longest x2 231 us: backward(): pl.pallas_call(kernel, grid=(steps,), in_specs=in_specs, out_specs=out_sp...]
    ppermute x0 -> x36, waiting for transfers between devices: none -> 41.2 us  [swap(): return lax.ppermute(v, 'dp', [(i, i ^ bit) for i in range(8)])]
    psum x1 -> x0, blocking collectives: 23 us -> none  [step(): total = lax.psum(jnp.sum(ssq1 + ssq0), 'dp')]
    ppermute x0 -> x36, starting transfers between devices: none -> 22 us  [swap(): return lax.ppermute(v, 'dp', [(i, i ^ bit) for i in range(8)])]
    squeeze x0 -> x8, local copies, waits for them, and re-layouts: none -> 7.41 us  [step(): p, q = (one[i][0][0], one[i][1][1])]
  transfers between devices with their start and end apart: 3 -> 36, of which waited for: 0 -> 13; matrix products, arithmetic and copies ran while one was open for 1% -> 1% of each run, Pallas kernels for 47% -> 40%
where the time goes in v2:
time: 494 us; the launch traced here: 493 us
  Pallas kernels  418 us (85%)
  waiting for transfers between devices  41.2 us (8%)
  starting transfers between devices  22 us (4%)
  local copies, waits for them, and re-layouts  10.8 us (2%)
    pallas_call x2, Pallas kernels, backward(): pl.pallas_call(kernel, grid=(steps,), in_specs=in_specs, out_specs=out_sp...  231 us
    pallas_call x8, Pallas kernels, optimizer(): pl.pallas_call(functools.partial(optimizer_kernel, len(gs), len(so_far)),...  137 us
    pallas_call x1, Pallas kernels, forward(): pl.pallas_call(forward_kernel, grid=(NT + NB,), in_specs=[whole((T, D)),...  49.9 us
    ppermute x36, waiting for transfers between devices, swap(): return lax.ppermute(v, 'dp', [(i, i ^ bit) for i in range(8)])  41.2 us
    ppermute x36, starting transfers between devices, swap(): return lax.ppermute(v, 'dp', [(i, i ^ bit) for i in range(8)])  22 us
  transfers between devices with their start and end apart: 36, of which 13 were waited for; matrix products, arithmetic and copies ran while one was open for 1% of the time, Pallas kernels for 40%

profile of v2, /device:TPU:0, one launch (start us, length us, event | category | flops | bytes accessed | tf_op | source)
XLA Modules:
  0.0 493.3 jit_solution(3037457623340925716)
XLA Ops:
  0.6 49.9 %forward.1 = (f32[11,2048,256]{2,1,0:T(8,128)}, f32[11,2048,256]{2,1,0:T(8,128)}, bf16[2048,1024]{1,0:T(8,128)(2,1)}, bf16[2048,1024]{1,0:T(8,128)(2,1)}, bf16[1...) custom-call(bf16[2048,1024]{1,0:T(8,128)(2,1)} %bitcast.18, ...), custom_call_target="tpu_custom_call" | custom-call | flops 35433480192 | bytes 104857600 | tf_op jit(solution)/shard_map/forward/pallas_call | solution.py:95
  50.6 133.6 %shard_map.178 = (bf16[2,4,3,128,128]{4,3,2,1,0:T(8,128)(2,1)}, bf16[2,5,3,128,128]{4,3,2,1,0:T(8,128)(2,1)}, bf16[2,2,8,3,128,128]{5,4,3,2,1,0:T(8,128)(2,1)}, ...) custom-call(bf16[2048,1024]{1,0:T(8,128)(2,1)} %get-tuple-element.17, ...), custom_call_target="tpu_custom_call" | custom-call | flops 94489280512 | bytes 67108864 | tf_op jit(solution)/shard_map/pallas_call | solution.py:478
  184.2 2.1 collective-permute-start
  186.3 1.5 collective-permute-start.1
  187.8 97.2 %shard_map.179 = (bf16[2,5,3,128,128]{4,3,2,1,0:T(8,128)(2,1)}, bf16[2,6,3,128,128]{4,3,2,1,0:T(8,128)(2,1)}, f32[8,128]{1,0:T(8,128)}) custom-call(bf16[2048,1024]{1,0:T(8,128)(2,1)} %get-tuple-element.178.dh_hbm, bf16[1024,2048]{1,0:T(8,128)(2,1)} %get-tuple-element.179.at_hbm, bf16[1024,2048]{1,0:T(8,128)(2,1)} %get-tuple-element.180.dht_hbm, ...), custom_call_target="tpu_custom_call" | custom-call | flops 47244640256 | bytes 67108864 | tf_op jit(solution)/shard_map/pallas_call | solution.py:478
  285.1 1.3 slice_bitcast_fusion.7
  286.4 1.2 collective-permute-start.2
  287.6 1.1 collective-permute-start.3
  289.9 7.7 %collective-permute-done.2.refs_3_ = bf16[4,3,128,128]{3,2,1,0:T(8,128)(2,1)} collective-permute-done((bf16[4,3,128,128]{3,2,1,0:T(8,128)(2,1)S(1)}, bf16[4,3,128,128]{3,2,1,0:T(8,128)(2,1)}, u32[]{:S(2)}, u32[]{:S(2)}) %collective-permute-start.2) | collective-permute-done | bytes 393248 | tf_op jit(solution)/shard_map/ppermute | solution.py:568
  297.6 1.2 collective-permute-start.10
  299.8 12.6 %shard_map.180 = (bf16[2,1024,2816]{2,1,0:T(8,128)(2,1)}, bf16[2,1024,2816]{2,1,0:T(8,128)(2,1)}, bf16[2,2816,1024]{2,1,0:T(8,128)(2,1)}, f32[2,1024,2816]{2,1,0...) custom-call(f32[8,128]{1,0:T(8,128)} %get-tuple-element.185.factor_r, ...), custom_call_target="tpu_custom_call" | custom-call | flops 1200000000 | bytes 34603008 | tf_op jit(solution)/shard_map/pallas_call | solution.py:540
  313.4 1.2 collective-permute-done.7.refs_8_
  315.2 12.0 %shard_map.181 = (bf16[2,1024,2816]{2,1,0:T(8,128)(2,1)}, bf16[2,1024,2816]{2,1,0:T(8,128)(2,1)}, bf16[2,2816,1024]{2,1,0:T(8,128)(2,1)}, f32[2,1024,2816]{2,1,0...) custom-call(f32[8,128]{1,0:T(8,128)} %get-tuple-element.185.factor_r, ...), custom_call_target="tpu_custom_call", output_to_operand_aliasing={{0}: (20, {}), {1}: (21, {}), {2}: (22, {}), {3}: (23, {}),... | custom-call | flops 1200000000 | bytes 34603008 | tf_op jit(solution)/shard_map/pallas_call | solution.py:540
  328.5 1.3 collective-permute-start.12
  329.8 11.2 %collective-permute-done.11.refs_3_ = bf16[5,3,128,128]{3,2,1,0:T(8,128)(2,1)} collective-permute-done((bf16[5,3,128,128]{3,2,1,0:T(8,128)(2,1)S(1)}, bf16[5,3,128,128]{3,2,1,0:T(8,128)(2,1)}, u32[]{:S(2)}, u32[]{:S(2)}) %collective-permute-start.11) | collective-permute-done | bytes 491552 | tf_op jit(solution)/shard_map/ppermute | solution.py:568
  341.0 1.1 collective-permute-start.18
  343.1 12.0 %shard_map.182 = (bf16[2,1024,2816]{2,1,0:T(8,128)(2,1)}, bf16[2,1024,2816]{2,1,0:T(8,128)(2,1)}, bf16[2,2816,1024]{2,1,0:T(8,128)(2,1)}, f32[2,1024,2816]{2,1,0...) custom-call(f32[8,128]{1,0:T(8,128)} %get-tuple-element.185.factor_r, ...), custom_call_target="tpu_custom_call", output_to_operand_aliasing={{0}: (20, {}), {1}: (21, {}), {2}: (22, {}), {3}: (23, {}),... | custom-call | flops 1200000000 | bytes 34603008 | tf_op jit(solution)/shard_map/pallas_call | solution.py:540
  355.8 1.6 collective-permute-done.16.refs_8_
  358.8 20.8 %shard_map.183 = (bf16[2,1024,2816]{2,1,0:T(8,128)(2,1)}, bf16[2,1024,2816]{2,1,0:T(8,128)(2,1)}, bf16[2,2816,1024]{2,1,0:T(8,128)(2,1)}, f32[2,1024,2816]{2,1,0...) custom-call(f32[8,128]{1,0:T(8,128)} %get-tuple-element.185.factor_r, ...), custom_call_target="tpu_custom_call", output_to_operand_aliasing={{0}: (20, {}), {1}: (21, {}), {2}: (22, {}), {3}: (23, {}),... | custom-call | flops 1800000000 | bytes 51904512 | tf_op jit(solution)/shard_map/pallas_call | solution.py:540
  379.6 1.1 slice_bitcast_fusion.3
  383.7 1.1 collective-permute-start.27
  384.8 9.1 %collective-permute-done.20.refs_3_ = bf16[5,3,128,128]{3,2,1,0:T(8,128)(2,1)S(1)} collective-permute-done((bf16[5,3,128,128]{3,2,1,0:T(8,128)(2,1)S(1)}, bf16[5,3,128,128]{3,2,1,0:T(8,128)(2,1)S(1)}, u32[]{:S(2)}, u32[]{:S(2)}) %collective-permute-start.20) | collective-permute-done | bytes 491552 | tf_op jit(solution)/shard_map/ppermute | solution.py:568
  394.9 1.9 collective-permute-done.21.refs_4_
  397.7 12.4 %shard_map.184 = (bf16[2,1024,2816]{2,1,0:T(8,128)(2,1)}, bf16[2,1024,2816]{2,1,0:T(8,128)(2,1)}, bf16[2,2816,1024]{2,1,0:T(8,128)(2,1)}, f32[2,1024,2816]{2,1,0...) custom-call(f32[8,128]{1,0:T(8,128)} %get-tuple-element.185.factor_r, ...), custom_call_target="tpu_custom_call", output_to_operand_aliasing={{0}: (20, {}), {1}: (21, {}), {2}: (22, {}), {3}: (23, {}),... | custom-call | flops 1200000000 | bytes 34603008 | tf_op jit(solution)/shard_map/pallas_call | solution.py:540
  410.6 1.8 collective-permute-done.25.refs_8_
  413.1 20.8 %shard_map.185 = (bf16[2,1024,2816]{2,1,0:T(8,128)(2,1)}, bf16[2,1024,2816]{2,1,0:T(8,128)(2,1)}, bf16[2,2816,1024]{2,1,0:T(8,128)(2,1)}, f32[2,1024,2816]{2,1,0...) custom-call(f32[8,128]{1,0:T(8,128)} %get-tuple-element.185.factor_r, ...), custom_call_target="tpu_custom_call", output_to_operand_aliasing={{0}: (20, {}), {1}: (21, {}), {2}: (22, {}), {3}: (23, {}),... | custom-call | flops 1800000000 | bytes 51904512 | tf_op jit(solution)/shard_map/pallas_call | solution.py:540
  433.9 1.9 slice_bitcast_fusion.1
  436.9 1.9 slice_bitcast_fusion
  440.1 12.0 %shard_map.186 = (bf16[2,1024,2816]{2,1,0:T(8,128)(2,1)}, bf16[2,1024,2816]{2,1,0:T(8,128)(2,1)}, bf16[2,2816,1024]{2,1,0:T(8,128)(2,1)}, f32[2,1024,2816]{2,1,0...) custom-call(f32[8,128]{1,0:T(8,128)} %get-tuple-element.185.factor_r, ...), custom_call_target="tpu_custom_call", output_to_operand_aliasing={{0}: (20, {}), {1}: (21, {}), {2}: (22, {}), {3}: (23, {}),... | custom-call | flops 1200000000 | bytes 34603008 | tf_op jit(solution)/shard_map/pallas_call | solution.py:540
  452.1 2.3 collective-permute-done.30.refs_4_
  455.0 1.5 collective-permute-done.34.refs_8_
  458.2 34.9 %shard_map.187 = (bf16[2,1024,2816]{2,1,0:T(8,128)(2,1)}, bf16[2,1024,2816]{2,1,0:T(8,128)(2,1)}, bf16[2,2816,1024]{2,1,0:T(8,128)(2,1)}, f32[2,1024,2816]{2,1,0...) custom-call(f32[8,128]{1,0:T(8,128)} %get-tuple-element.185.factor_r, ...), custom_call_target="tpu_custom_call", output_to_operand_aliasing={{0}: (20, {}), {1}: (21, {}), {2}: (22, {}), {3}: (23, {}),... | custom-call | flops 3600000000 | bytes 103809024 | tf_op jit(solution)/shard_map/pallas_call | solution.py:540
  (83 shorter events, 18.7 us)
Async XLA Ops:
  184.2 100.9 %collective-permute-start = (bf16[2,4,3,128,128]{4,3,2,1,0:T(8,128)(2,1)}, bf16[2,4,3,128,128]{4,3,2,1,0:T(8,128)(2,1)}, u32[]{:S(2)}, u32[]{:S(2)}) collective-permute-start(bf16[2,4,3,128,128]{4,3,2,1,0:T(8,128)(2,1)} %get-tuple-element.187.refs_0_), channel_id=1, source_target_pairs={{0,2},{1,3},{2,0},{3,1},{4,6},{5,7},{6,4},{7,5}} | collective-permute-start | bytes 2359304 | tf_op jit(solution)/shard_map/ppermute | solution.py:568
  186.3 98.8 %collective-permute-start.1 = (bf16[2,4,3,128,128]{4,3,2,1,0:T(8,128)(2,1)}, bf16[2,4,3,128,128]{4,3,2,1,0:T(8,128)(2,1)S(1)}, u32[]{:S(2)}, u32[]{:S(2)}) collective-permute-start(bf16[2,4,3,128,128]{4,3,2,1,0:T(8,128)(2,1)} %get-tuple-element.187.refs_0_), channel_id=1, source_target_pairs={{0,4},{1,5},{2,6},{3,7},{4,0},{5,1},{6,2},{7,3}} | collective-permute-start | bytes 2359304 | tf_op jit(solution)/shard_map/ppermute | solution.py:568
  286.4 11.3 %collective-permute-start.2 = (bf16[4,3,128,128]{3,2,1,0:T(8,128)(2,1)S(1)}, bf16[4,3,128,128]{3,2,1,0:T(8,128)(2,1)}, u32[]{:S(2)}, u32[]{:S(2)}) collective-permute-start(bf16[4,3,128,128]{3,2,1,0:T(8,128)(2,1)S(1)} %slice_bitcast_fusion.7), channel_id=1, source_target_pairs={{0,4},{1,5},{2,6},{3,7},{4,0},{5,1},{6,2},{7,3}} | collective-permute-start | bytes 1179656 | tf_op jit(solution)/shard_map/ppermute | solution.py:568
  287.6 24.8 %collective-permute-start.4 = (bf16[2,4,3,128,128]{4,3,2,1,0:T(8,128)(2,1)}, bf16[2,4,3,128,128]{4,3,2,1,0:T(8,128)(2,1)}, u32[]{:S(2)}, u32[]{:S(2)}) collective-permute-start(bf16[2,4,3,128,128]{4,3,2,1,0:T(8,128)(2,1)} %get-tuple-element.187.refs_0_), channel_id=1, source_target_pairs={{0,1},{1,0},{2,3},{3,2},{4,5},{5,4},{6,7},{7,6}} | collective-permute-start | bytes 2359304 | tf_op jit(solution)/shard_map/ppermute | solution.py:568
  287.6 12.1 %collective-permute-start.3 = (bf16[4,3,128,128]{3,2,1,0:T(8,128)(2,1)S(1)}, bf16[4,3,128,128]{3,2,1,0:T(8,128)(2,1)}, u32[]{:S(2)}, u32[]{:S(2)}) collective-permute-start(bf16[4,3,128,128]{3,2,1,0:T(8,128)(2,1)S(1)} %slice_bitcast_fusion.6), channel_id=1, source_target_pairs={{0,2},{1,3},{2,0},{3,1},{4,6},{5,7},{6,4},{7,5}} | collective-permute-start | bytes 1179656 | tf_op jit(solution)/shard_map/ppermute | solution.py:568
  288.8 24.1 %collective-permute-start.5 = (bf16[2,4,3,128,128]{4,3,2,1,0:T(8,128)(2,1)}, bf16[2,4,3,128,128]{4,3,2,1,0:T(8,128)(2,1)}, u32[]{:S(2)}, u32[]{:S(2)}) collective-permute-start(bf16[2,4,3,128,128]{4,3,2,1,0:T(8,128)(2,1)} %collective-permute-done.refs_1_), channel_id=1, source_target_pairs={{0,1},{1,0},{2,3},{3,2},{4,5},{5,4},{6,7},{7,6}} | collective-permute-start | bytes 2359304 | tf_op jit(solution)/shard_map/ppermute | solution.py:568
  289.0 38.2 %collective-permute-start.9 = (bf16[2,5,3,128,128]{4,3,2,1,0:T(8,128)(2,1)}, bf16[2,5,3,128,128]{4,3,2,1,0:T(8,128)(2,1)S(1)}, u32[]{:S(2)}, u32[]{:S(2)}) collective-permute-start(bf16[2,5,3,128,128]{4,3,2,1,0:T(8,128)(2,1)} %get-tuple-element.186.refs_0_), channel_id=1, source_target_pairs={{0,2},{1,3},{2,0},{3,1},{4,6},{5,7},{6,4},{7,5}} | collective-permute-start | bytes 2949128 | tf_op jit(solution)/shard_map/ppermute | solution.py:568
  297.6 29.5 %collective-permute-start.10 = (bf16[2,5,3,128,128]{4,3,2,1,0:T(8,128)(2,1)}, bf16[2,5,3,128,128]{4,3,2,1,0:T(8,128)(2,1)S(1)}, u32[]{:S(2)}, u32[]{:S(2)}) collective-permute-start(bf16[2,5,3,128,128]{4,3,2,1,0:T(8,128)(2,1)} %get-tuple-element.186.refs_0_), channel_id=1, source_target_pairs={{0,4},{1,5},{2,6},{3,7},{4,0},{5,1},{6,2},{7,3}} | collective-permute-start | bytes 2949128 | tf_op jit(solution)/shard_map/ppermute | solution.py:568
  299.8 13.2 %collective-permute-start.6 = (bf16[2,4,3,128,128]{4,3,2,1,0:T(8,128)(2,1)}, bf16[2,4,3,128,128]{4,3,2,1,0:T(8,128)(2,1)}, u32[]{:S(2)}, u32[]{:S(2)}) collective-permute-start(bf16[2,4,3,128,128]{4,3,2,1,0:T(8,128)(2,1)} %copy-done.2), channel_id=1, source_target_pairs={{0,1},{1,0},{2,3},{3,2},{4,5},{5,4},{6,7},{7,6}} | collective-permute-start | bytes 2359304 | tf_op jit(solution)/shard_map/ppermute | solution.py:568
  313.0 42.2 %collective-permute-start.13 = (bf16[2,5,3,128,128]{4,3,2,1,0:T(8,128)(2,1)}, bf16[2,5,3,128,128]{4,3,2,1,0:T(8,128)(2,1)}, u32[]{:S(2)}, u32[]{:S(2)}) collective-permute-start(bf16[2,5,3,128,128]{4,3,2,1,0:T(8,128)(2,1)} %get-tuple-element.186.refs_0_), channel_id=1, source_target_pairs={{0,1},{1,0},{2,3},{3,2},{4,5},{5,4},{6,7},{7,6}} | collective-permute-start | bytes 2949128 | tf_op jit(solution)/shard_map/ppermute | solution.py:568
  327.2 28.0 %collective-permute-start.14 = (bf16[2,5,3,128,128]{4,3,2,1,0:T(8,128)(2,1)S(1)}, bf16[2,5,3,128,128]{4,3,2,1,0:T(8,128)(2,1)}, u32[]{:S(2)}, u32[]{:S(2)}) collective-permute-start(bf16[2,5,3,128,128]{4,3,2,1,0:T(8,128)(2,1)S(1)} %collective-permute-done.9.refs_1_), channel_id=1, source_target_pairs={{0,1},{1,0},{2,3},{3,2},{4,5},{5,4},{6,7},{7,6}} | collective-permute-start | bytes 2949128 | tf_op jit(solution)/shard_map/ppermute | solution.py:568
  327.6 13.4 %collective-permute-start.11 = (bf16[5,3,128,128]{3,2,1,0:T(8,128)(2,1)S(1)}, bf16[5,3,128,128]{3,2,1,0:T(8,128)(2,1)}, u32[]{:S(2)}, u32[]{:S(2)}) collective-permute-start(bf16[5,3,128,128]{3,2,1,0:T(8,128)(2,1)S(1)} %slice_bitcast_fusion.5), channel_id=1, source_target_pairs={{0,4},{1,5},{2,6},{3,7},{4,0},{5,1},{6,2},{7,3}} | collective-permute-start | bytes 1474568 | tf_op jit(solution)/shard_map/ppermute | solution.py:568
  328.5 13.6 %collective-permute-start.12 = (bf16[5,3,128,128]{3,2,1,0:T(8,128)(2,1)S(1)}, bf16[5,3,128,128]{3,2,1,0:T(8,128)(2,1)}, u32[]{:S(2)}, u32[]{:S(2)}) collective-permute-start(bf16[5,3,128,128]{3,2,1,0:T(8,128)(2,1)S(1)} %slice_bitcast_fusion.4), channel_id=1, source_target_pairs={{0,2},{1,3},{2,0},{3,1},{4,6},{5,7},{6,4},{7,5}} | collective-permute-start | bytes 1474568 | tf_op jit(solution)/shard_map/ppermute | solution.py:568
  329.8 25.9 %collective-permute-start.15 = (bf16[2,5,3,128,128]{4,3,2,1,0:T(8,128)(2,1)S(1)}, bf16[2,5,3,128,128]{4,3,2,1,0:T(8,128)(2,1)}, u32[]{:S(2)}, u32[]{:S(2)}) collective-permute-start(bf16[2,5,3,128,128]{4,3,2,1,0:T(8,128)(2,1)S(1)} %collective-permute-done.10.refs_2_), channel_id=1, source_target_pairs={{0,1},{1,0},{2,3},{3,2},{4,5},{5,4},{6,7},{7,6}} | collective-permute-start | bytes 2949128 | tf_op jit(solution)/shard_map/ppermute | solution.py:568
  341.0 38.5 %collective-permute-start.18 = (bf16[2,5,3,128,128]{4,3,2,1,0:T(8,128)(2,1)}, bf16[2,5,3,128,128]{4,3,2,1,0:T(8,128)(2,1)}, u32[]{:S(2)}, u32[]{:S(2)}) collective-permute-start(bf16[2,5,3,128,128]{4,3,2,1,0:T(8,128)(2,1)} %get-tuple-element.261.refs_0_), channel_id=1, source_target_pairs={{0,2},{1,3},{2,0},{3,1},{4,6},{5,7},{6,4},{7,5}} | collective-permute-start | bytes 2949128 | tf_op jit(solution)/shard_map/ppermute | solution.py:568
  342.1 37.4 %collective-permute-start.19 = (bf16[2,5,3,128,128]{4,3,2,1,0:T(8,128)(2,1)}, bf16[2,5,3,128,128]{4,3,2,1,0:T(8,128)(2,1)}, u32[]{:S(2)}, u32[]{:S(2)}) collective-permute-start(bf16[2,5,3,128,128]{4,3,2,1,0:T(8,128)(2,1)} %get-tuple-element.261.refs_0_), channel_id=1, source_target_pairs={{0,4},{1,5},{2,6},{3,7},{4,0},{5,1},{6,2},{7,3}} | collective-permute-start | bytes 2949128 | tf_op jit(solution)/shard_map/ppermute | solution.py:568
  355.2 2.8 collective-permute-start.17
  355.7 54.3 %collective-permute-start.22 = (bf16[2,5,3,128,128]{4,3,2,1,0:T(8,128)(2,1)}, bf16[2,5,3,128,128]{4,3,2,1,0:T(8,128)(2,1)}, u32[]{:S(2)}, u32[]{:S(2)}) collective-permute-start(bf16[2,5,3,128,128]{4,3,2,1,0:T(8,128)(2,1)} %get-tuple-element.261.refs_0_), channel_id=1, source_target_pairs={{0,1},{1,0},{2,3},{3,2},{4,5},{5,4},{6,7},{7,6}} | collective-permute-start | bytes 2949128 | tf_op jit(solution)/shard_map/ppermute | solution.py:568
  380.6 13.3 %collective-permute-start.20 = (bf16[5,3,128,128]{3,2,1,0:T(8,128)(2,1)S(1)}, bf16[5,3,128,128]{3,2,1,0:T(8,128)(2,1)S(1)}, u32[]{:S(2)}, u32[]{:S(2)}) collective-permute-start(bf16[5,3,128,128]{3,2,1,0:T(8,128)(2,1)S(1)} %slice_bitcast_fusion.3), channel_id=1, source_target_pairs={{0,4},{1,5},{2,6},{3,7},{4,0},{5,1},{6,2},{7,3}} | collective-permute-start | bytes 1474568 | tf_op jit(solution)/shard_map/ppermute | solution.py:568
  382.7 14.1 %collective-permute-start.21 = (bf16[5,3,128,128]{3,2,1,0:T(8,128)(2,1)S(1)}, bf16[5,3,128,128]{3,2,1,0:T(8,128)(2,1)S(1)}, u32[]{:S(2)}, u32[]{:S(2)}) collective-permute-start(bf16[5,3,128,128]{3,2,1,0:T(8,128)(2,1)S(1)} %slice_bitcast_fusion.2), channel_id=1, source_target_pairs={{0,2},{1,3},{2,0},{3,1},{4,6},{5,7},{6,4},{7,5}} | collective-permute-start | bytes 1474568 | tf_op jit(solution)/shard_map/ppermute | solution.py:568
  383.7 26.9 %collective-permute-start.23 = (bf16[2,5,3,128,128]{4,3,2,1,0:T(8,128)(2,1)}, bf16[2,5,3,128,128]{4,3,2,1,0:T(8,128)(2,1)S(1)}, u32[]{:S(2)}, u32[]{:S(2)}) collective-permute-start(bf16[2,5,3,128,128]{4,3,2,1,0:T(8,128)(2,1)} %collective-permute-done.18.refs_1_), channel_id=1, source_target_pairs={{0,1},{1,0},{2,3},{3,2},{4,5},{5,4},{6,7},{7,6}} | collective-permute-start | bytes 2949128 | tf_op jit(solution)/shard_map/ppermute | solution.py:568
  383.7 50.2 %collective-permute-start.27 = (bf16[2,6,3,128,128]{4,3,2,1,0:T(8,128)(2,1)}, bf16[2,6,3,128,128]{4,3,2,1,0:T(8,128)(2,1)}, u32[]{:S(2)}, u32[]{:S(2)}) collective-permute-start(bf16[2,6,3,128,128]{4,3,2,1,0:T(8,128)(2,1)} %get-tuple-element.263.refs_0_), channel_id=1, source_target_pairs={{0,2},{1,3},{2,0},{3,1},{4,6},{5,7},{6,4},{7,5}} | collective-permute-start | bytes 3538952 | tf_op jit(solution)/shard_map/ppermute | solution.py:568
  393.9 40.0 %collective-permute-start.28 = (bf16[2,6,3,128,128]{4,3,2,1,0:T(8,128)(2,1)}, bf16[2,6,3,128,128]{4,3,2,1,0:T(8,128)(2,1)}, u32[]{:S(2)}, u32[]{:S(2)}) collective-permute-start(bf16[2,6,3,128,128]{4,3,2,1,0:T(8,128)(2,1)} %get-tuple-element.263.refs_0_), channel_id=1, source_target_pairs={{0,4},{1,5},{2,6},{3,7},{4,0},{5,1},{6,2},{7,3}} | collective-permute-start | bytes 3538952 | tf_op jit(solution)/shard_map/ppermute | solution.py:568
  397.7 13.0 %collective-permute-start.24 = (bf16[2,5,3,128,128]{4,3,2,1,0:T(8,128)(2,1)}, bf16[2,5,3,128,128]{4,3,2,1,0:T(8,128)(2,1)S(1)}, u32[]{:S(2)}, u32[]{:S(2)}) collective-permute-start(bf16[2,5,3,128,128]{4,3,2,1,0:T(8,128)(2,1)} %collective-permute-done.19.refs_2_), channel_id=1, source_target_pairs={{0,1},{1,0},{2,3},{3,2},{4,5},{5,4},{6,7},{7,6}} | collective-permute-start | bytes 2949128 | tf_op jit(solution)/shard_map/ppermute | solution.py:568
  410.0 2.4 collective-permute-start.25
  410.6 2.5 collective-permute-start.26
  435.9 16.3 %collective-permute-start.29 = (bf16[6,3,128,128]{3,2,1,0:T(8,128)(2,1)}, bf16[6,3,128,128]{3,2,1,0:T(8,128)(2,1)S(1)}, u32[]{:S(2)}, u32[]{:S(2)}) collective-permute-start(bf16[6,3,128,128]{3,2,1,0:T(8,128)(2,1)} %slice_bitcast_fusion.1), channel_id=1, source_target_pairs={{0,4},{1,5},{2,6},{3,7},{4,0},{5,1},{6,2},{7,3}} | collective-permute-start | bytes 1769480 | tf_op jit(solution)/shard_map/ppermute | solution.py:568
  438.8 15.6 %collective-permute-start.30 = (bf16[6,3,128,128]{3,2,1,0:T(8,128)(2,1)}, bf16[6,3,128,128]{3,2,1,0:T(8,128)(2,1)}, u32[]{:S(2)}, u32[]{:S(2)}) collective-permute-start(bf16[6,3,128,128]{3,2,1,0:T(8,128)(2,1)} %slice_bitcast_fusion), channel_id=1, source_target_pairs={{0,2},{1,3},{2,0},{3,1},{4,6},{5,7},{6,4},{7,5}} | collective-permute-start | bytes 1769480 | tf_op jit(solution)/shard_map/ppermute | solution.py:568
  439.6 15.4 %collective-permute-start.31 = (bf16[2,6,3,128,128]{4,3,2,1,0:T(8,128)(2,1)}, bf16[2,6,3,128,128]{4,3,2,1,0:T(8,128)(2,1)S(1)}, u32[]{:S(2)}, u32[]{:S(2)}) collective-permute-start(bf16[2,6,3,128,128]{4,3,2,1,0:T(8,128)(2,1)} %get-tuple-element.263.refs_0_), channel_id=1, source_target_pairs={{0,1},{1,0},{2,3},{3,2},{4,5},{5,4},{6,7},{7,6}} | collective-permute-start | bytes 3538952 | tf_op jit(solution)/shard_map/ppermute | solution.py:568
  439.6 18.6 %collective-permute-start.32 = (bf16[2,6,3,128,128]{4,3,2,1,0:T(8,128)(2,1)}, bf16[2,6,3,128,128]{4,3,2,1,0:T(8,128)(2,1)}, u32[]{:S(2)}, u32[]{:S(2)}) collective-permute-start(bf16[2,6,3,128,128]{4,3,2,1,0:T(8,128)(2,1)} %collective-permute-done.27.refs_1_), channel_id=1, source_target_pairs={{0,1},{1,0},{2,3},{3,2},{4,5},{5,4},{6,7},{7,6}} | collective-permute-start | bytes 3538952 | tf_op jit(solution)/shard_map/ppermute | solution.py:568
  440.1 18.1 %collective-permute-start.33 = (bf16[2,6,3,128,128]{4,3,2,1,0:T(8,128)(2,1)}, bf16[2,6,3,128,128]{4,3,2,1,0:T(8,128)(2,1)}, u32[]{:S(2)}, u32[]{:S(2)}) collective-permute-start(bf16[2,6,3,128,128]{4,3,2,1,0:T(8,128)(2,1)} %collective-permute-done.28.refs_2_), channel_id=1, source_target_pairs={{0,1},{1,0},{2,3},{3,2},{4,5},{5,4},{6,7},{7,6}} | collective-permute-start | bytes 3538952 | tf_op jit(solution)/shard_map/ppermute | solution.py:568
  454.5 2.9 collective-permute-start.35
  (16 other events, 87.0 us)
